TPU v7x, 1024 devices: a whole 4x8x16 slice. The times are simulated.
1024 devices in a mesh: gx: 16 (over y, core), gy: 16 (over z), gz: 4 (over x).
Axes of the slice: x: 4, y: 8, z: 16, core: 2. Of those that a mesh axis runs over, the one named last changes fastest.
Arguments:
- rhs: float32 [4, 128, 128, 512], P(None, 'gx', 'gy', 'gz'), may hold values from -170 to 170
- basis: bfloat16 [4, 8, 128, 128, 512], P(None, None, 'gx', 'gy', 'gz'), may hold values from -6 to 6
- inertia: float32 [128, 128, 512], P('gx', 'gy', 'gz'), may hold values from 0.5 to 2
- helm: float32 [4], replicated, may hold values from 0.2 to 1
- stiffness: float32 [8, 8], replicated, may hold values from -0.05 to 0.6, as said below
Outputs:
- solution: float32 [4, 128, 128, 512], P(None, 'gx', 'gy', 'gz')
- new_basis: bfloat16 [4, 128, 128, 512], P(None, 'gx', 'gy', 'gz')
Inputs may be any that keep to these rules, and one draw needn't show every extreme that they name: `stiffness`: symmetric; every diagonal entry exceeds the sum of the magnitudes of the other entries of its row.
All inputs are finite; a program needn't handle non-finite values.
Results may differ from a plain program's by a relative error of at most 0.001.
Values sent between devices are 32-bit elements; how exact they have to be, the bound alone decides.
No kernel may reach another device: no remote copies, remote signals or barrier semaphores. Data moves between devices by JAX's collectives and lax.ppermute only.
A program may use at most 32 MiB of HBM per device.

v0:
```python
import functools

import jax
import jax.numpy as jnp
from jax import lax
from jax.sharding import Mesh
from jax.sharding import PartitionSpec as P

ITERS = 2
GX = ("gx_0", "gx_1")
GX_GY_GZ = ("gx_0", "gx_1", "gy", "gz")


penalty = 0.15
epsilon = 1e-06
highest = lax.Precision.HIGHEST


def extended(x, sides, width):
    edges = {}
    for axis, dim in sides:
        count, length = (lax.axis_size(axis), x.shape[dim])
        up = [(i, (i + 1) % count) for i in range(count - 1)]
        last = lax.slice_in_dim(x, length - width, length, axis=dim)
        leading = lax.slice_in_dim(x, 0, width, axis=dim)
        edges[dim] = (
            lax.ppermute(last, axis, up),
            lax.ppermute(leading, axis, [(b, a) for a, b in up]),
        )
    done = []
    for _, dim in sides:
        low, high = edges[dim]
        around = [(width, width) if d in done else (0, 0) for d in range(x.ndim)]
        x = jnp.concatenate([jnp.pad(low, around), x, jnp.pad(high, around)], axis=dim)
        done.append(dim)
    return x


def by_axis(x, axes):
    return functools.reduce(lax.psum, axes, x)


def block_matrix(stiffness, size_c):
    points = stiffness.shape[0]
    cells = lax.broadcasted_iota(jnp.int32, (size_c, points), 0)
    slots = lax.broadcasted_iota(jnp.int32, (size_c, points), 1)
    selector = jnp.where(cells % points == slots, 1.0, 0.0).astype(jnp.float32)
    spread_out = jnp.dot(
        jnp.dot(selector, stiffness, precision=highest), selector.T, precision=highest
    )
    rows_block = lax.broadcasted_iota(jnp.int32, (size_c, size_c), 0) // points
    cols_block = lax.broadcasted_iota(jnp.int32, (size_c, size_c), 1) // points
    return jnp.where(rows_block == cols_block, spread_out, 0.0)


def stiffen(vector, stiffness, full_block):
    leading, size_a, size_b, size_c = vector.shape
    points = stiffness.shape[0]
    along_a = jnp.einsum(
        "ij,sajbc->saibc",
        stiffness,
        vector.reshape(leading, size_a // points, points, size_b, size_c),
        precision=highest,
    ).reshape(vector.shape)
    along_b = jnp.einsum(
        "ij,sabjc->sabic",
        stiffness,
        vector.reshape(leading, size_a, size_b // points, points, size_c),
        precision=highest,
    ).reshape(vector.shape)
    along_c = jnp.einsum("sabj,ij->sabi", vector, full_block, precision=highest)
    return along_a + along_b + along_c


def face_terms(vector, padded, points):
    accumulated = jnp.zeros_like(vector)
    neighbours = (
        (1, padded[:, 2:, 1:-1, 1:-1], padded[:, :-2, 1:-1, 1:-1]),
        (2, padded[:, 1:-1, 2:, 1:-1], padded[:, 1:-1, :-2, 1:-1]),
        (3, padded[:, 1:-1, 1:-1, 2:], padded[:, 1:-1, 1:-1, :-2]),
    )
    for axis_pos, higher, lower_side in neighbours:
        position = lax.broadcasted_iota(jnp.int32, vector.shape, axis_pos) % points
        accumulated = accumulated + jnp.where(position == points - 1, vector - higher, 0.0)
        accumulated = accumulated + jnp.where(position == 0, vector - lower_side, 0.0)
    return accumulated


def operate(vector, padded, diagonal, stiffness, full_block):
    return (
        diagonal * vector
        + stiffen(vector, stiffness, full_block)
        + penalty * face_terms(vector, padded, stiffness.shape[0])
    )


def per_solve(values):
    return values[:, None, None, None]


def on_device(rhs, basis, inertia, helm, stiffness):
    point_count = float(rhs[0].size * lax.axis_size(GX) * lax.axis_size("gy") * lax.axis_size("gz"))
    diagonal = helm[:, None, None, None] * inertia[None]
    full_block = block_matrix(stiffness, rhs.shape[3])

    def apply_all(vector):
        padded = extended(vector, ((GX, 1), ("gy", 2), ("gz", 3)), 1)
        return operate(vector, padded, diagonal, stiffness, full_block)

    def combine(weights):
        return jnp.einsum("sk,skxyz->sxyz", weights, basis, precision=highest)

    local_coef = jnp.einsum("skxyz,sxyz->sk", basis, rhs, precision=highest)
    local_gram = jnp.einsum("skxyz,slxyz->skl", basis, basis, preferred_element_type=jnp.float32)
    coef_sum, gram_sum = (by_axis(local_coef, GX_GY_GZ), by_axis(local_gram, GX_GY_GZ))
    gram_matrix = gram_sum / point_count
    iterate = combine(coef_sum / point_count)
    residual = rhs - apply_all(iterate)
    direction = jnp.zeros_like(rhs)
    image_dir = jnp.zeros_like(rhs)
    norm_old = None
    step_old = None
    final_moment = None
    final_square = None
    for iteration in range(ITERS):
        image_vec = apply_all(residual)
        norm_part = jnp.sum(residual * residual, axis=(1, 2, 3))
        curv_part = jnp.sum(residual * image_vec, axis=(1, 2, 3))
        folding = False
        if iteration < ITERS - 1:
            norm_now, curvature = (by_axis(norm_part, GX_GY_GZ), by_axis(curv_part, GX_GY_GZ))
        else:
            folding = True
            triple = jnp.stack([iterate, residual, direction], axis=1)
            moment_part = jnp.einsum("skxyz,smxyz->smk", basis, triple, precision=highest)
            self_part = jnp.sum(iterate * iterate, axis=(1, 2, 3))
            cross_resid = jnp.sum(iterate * residual, axis=(1, 2, 3))
            cross_dir = jnp.sum(iterate * direction, axis=(1, 2, 3))
            resid_dir = jnp.sum(residual * direction, axis=(1, 2, 3))
            dir_square = jnp.sum(direction * direction, axis=(1, 2, 3))
            (
                norm_now,
                curvature,
                moments,
                self_sum,
                cross_resid,
                cross_dir,
                resid_dir,
                dir_square,
            ) = (
                by_axis(norm_part, GX_GY_GZ),
                by_axis(curv_part, GX_GY_GZ),
                by_axis(moment_part, GX_GY_GZ),
                by_axis(self_part, GX_GY_GZ),
                by_axis(cross_resid, GX_GY_GZ),
                by_axis(cross_dir, GX_GY_GZ),
                by_axis(resid_dir, GX_GY_GZ),
                by_axis(dir_square, GX_GY_GZ),
            )
        if iteration == 0:
            conjugacy = jnp.zeros_like(norm_now)
            step_size = norm_now / curvature
        else:
            conjugacy = norm_now / norm_old
            step_size = norm_now / (curvature - conjugacy * norm_now / step_old)
        if folding:
            final_moment = moments[:, 0, :] + step_size[:, None] * (
                moments[:, 1, :] + conjugacy[:, None] * moments[:, 2, :]
            )
            final_square = (
                self_sum
                + 2.0 * step_size * (cross_resid + conjugacy * cross_dir)
                + step_size
                * step_size
                * (norm_now + 2.0 * conjugacy * resid_dir + conjugacy * conjugacy * dir_square)
            )
        direction = residual + per_solve(conjugacy) * direction
        image_dir = image_vec + per_solve(conjugacy) * image_dir
        iterate = iterate + per_solve(step_size) * direction
        if iteration < ITERS - 1:
            residual = residual - per_solve(step_size) * image_dir
        norm_old = norm_now
        step_old = step_size
    weights = final_moment / point_count
    square = final_square / point_count
    spread = (
        square
        - 2.0 * jnp.sum(weights * weights, axis=1)
        + jnp.einsum("sk,skl,sl->s", weights, gram_matrix, weights, precision=highest)
    )
    remainder = iterate - combine(weights)
    new_basis = (remainder * per_solve(lax.rsqrt(spread + epsilon))).astype(jnp.bfloat16)
    return (iterate, new_basis)


def solution(mesh):
    torus = Mesh(
        mesh.devices.reshape(8, 2, mesh.shape["gy"], mesh.shape["gz"]), ("gx_0", "gx_1", "gy", "gz")
    )
    placed = (P(None, GX, "gy", "gz"), P(None, None, GX, "gy", "gz"), P(GX, "gy", "gz"), P(), P())
    return jax.shard_map(
        on_device,
        mesh=torus,
        in_specs=placed,
        out_specs=(P(None, GX, "gy", "gz"), P(None, GX, "gy", "gz")),
        check_vma=False,
    )
```

profile of v0, /device:TPU:4, one launch (start us, length us, event | category | flops | bytes accessed | tf_op | source)
XLA Modules:
  0.0 296.4 jit_solution(9630092688062602713)
XLA Ops:
  0.6 0.0 copy-start
  0.7 2.6 fusion.19
  3.3 17.6 %psum.320 = f32[4,8]{1,0:T(4,128)S(1)} all-reduce(f32[4,8]{1,0:T(4,128)S(1)} %bitcast.140), channel_id=1, replica_groups=mesh['gx_0'=8,'gx_1'=2,'gy'=16,'gz'=4] {'gx_0'}, use_global_device_ids=true, to_apply=%region_0.1 | all-reduce | flops 32 | bytes 256 | tf_op jit(solution)/shard_map/psum | solution.py:40
  20.9 2.5 psum.321
  23.4 43.3 %psum.322 = f32[4,8]{1,0:T(4,128)S(1)} all-reduce(f32[4,8]{1,0:T(4,128)S(1)} %psum.321), channel_id=1, replica_groups=mesh['gx_0'=8,'gx_1'=2,'gy'=16,'gz'=4] {'gy'}, use_global_device_ids=true, to_apply=%region_2.3 | all-reduce | flops 32 | bytes 256 | tf_op jit(solution)/shard_map/psum | solution.py:40
  66.7 8.3 %psum.323 = f32[4,8]{1,0:T(4,128)S(1)} all-reduce(f32[4,8]{1,0:T(4,128)S(1)} %psum.322), channel_id=1, replica_groups=mesh['gx_0'=8,'gx_1'=2,'gy'=16,'gz'=4] {'gz'}, use_global_device_ids=true, to_apply=%region_3.4 | all-reduce | flops 32 | bytes 256 | tf_op jit(solution)/shard_map/psum | solution.py:40
  75.0 0.7 fusion.17
  75.8 0.1 fusion.122
  75.9 2.7 collective-permute-start.4
  78.6 3.2 %collective-permute-start.5 = (f32[4,8,8,1]{3,1,2,0:T(8,128)S(1)}, f32[4,8,8,1]{3,1,2,0:T(8,128)S(1)}, u32[]{:S(2)}, u32[]{:S(2)}) collective-permute-start(f32[4,8,8,1]{3,1,2,0:T(8,128)S(1)} %get-tuple-element.72), channel_id=1, source_target_pairs={{0,1},{1,2},{2,3},{4,5},{5,6},{6,7},{8,9},{9,10},{10,11},{12,13},{... | collective-permute-start | bytes 3080 | tf_op jit(solution)/shard_map/ppermute | solution.py:27
  81.7 1.3 collective-permute-start.2
  83.0 4.5 %collective-permute-start.3 = (f32[4,8,1,128]{3,1,2,0:T(8,128)S(1)}, f32[4,8,1,128]{3,1,2,0:T(8,128)S(1)}, u32[]{:S(2)}, u32[]{:S(2)}) collective-permute-start(f32[4,8,1,128]{3,1,2,0:T(8,128)S(1)} %get-tuple-element.75), channel_id=1, source_target_pairs={{0,4},{4,8},{8,12},{12,16},{16,20},{20,24},{24,28},{28,32},{32,36}... | collective-permute-start | bytes 49160 | tf_op jit(solution)/shard_map/ppermute | solution.py:27
  87.6 1.3 collective-permute-start
  89.0 0.5 convolution_bitcast_fusion.3
  89.5 0.3 fusion.108
  89.8 0.3 fusion.2
  90.0 0.3 fusion.89
  90.3 0.0 copy-start.2
  90.3 0.4 fusion.12
  90.7 0.0 copy-start.3
  90.7 3.2 %collective-permute-start.1 = (f32[4,1,8,128]{3,1,2,0:T(1,128)S(1)}, f32[4,1,8,128]{3,1,2,0:T(1,128)S(1)}, u32[]{:S(2)}, u32[]{:S(2)}) collective-permute-start(f32[4,1,8,128]{3,1,2,0:T(1,128)S(1)} %get-tuple-element.73), channel_id=1, source_target_pairs={{0,64},{64,128},{128,192},{192,256},{256,320},{320,384},{384,448},... | collective-permute-start | bytes 49160 | tf_op jit(solution)/shard_map/ppermute | solution.py:27
  94.0 0.0 copy-start.4
  94.0 0.0 collective-permute-done.3
  94.0 0.7 collective-permute-done.1
  94.7 0.4 fusion.5
  95.1 0.3 fusion.86
  95.4 0.1 fusion.119
  95.5 1.3 collective-permute-start.8
  96.8 3.1 %collective-permute-start.10 = (f32[4,8,8,1]{3,1,2,0:T(8,128)S(1)}, f32[4,8,8,1]{3,1,2,0:T(8,128)S(1)}, u32[]{:S(2)}, u32[]{:S(2)}) collective-permute-start(f32[4,8,8,1]{3,1,2,0:T(8,128)S(1)} %get-tuple-element.65), channel_id=1, source_target_pairs={{1,0},{2,1},{3,2},{5,4},{6,5},{7,6},{9,8},{10,9},{11,10},{13,12},{... | collective-permute-start | bytes 3080 | tf_op jit(solution)/shard_map/ppermute | solution.py:28
  99.9 2.8 collective-permute-start.11
  102.7 4.5 %collective-permute-start.9 = (f32[4,8,1,128]{3,1,2,0:T(8,128)S(1)}, f32[4,8,1,128]{3,1,2,0:T(8,128)S(1)}, u32[]{:S(2)}, u32[]{:S(2)}) collective-permute-start(f32[4,8,1,128]{3,1,2,0:T(8,128)S(1)} %get-tuple-element.69), channel_id=1, source_target_pairs={{0,4},{4,8},{8,12},{12,16},{16,20},{20,24},{24,28},{28,32},{32,36}... | collective-permute-start | bytes 49160 | tf_op jit(solution)/shard_map/ppermute | solution.py:27
  107.3 1.3 collective-permute-start.6
  108.6 3.0 %collective-permute-start.7 = (f32[4,1,8,128]{3,1,2,0:T(1,128)S(1)}, f32[4,1,8,128]{3,1,2,0:T(1,128)S(1)}, u32[]{:S(2)}, u32[]{:S(2)}) collective-permute-start(f32[4,1,8,128]{3,1,2,0:T(1,128)S(1)} %get-tuple-element.67), channel_id=1, source_target_pairs={{0,64},{64,128},{128,192},{192,256},{256,320},{320,384},{384,448},... | collective-permute-start | bytes 49160 | tf_op jit(solution)/shard_map/ppermute | solution.py:27
  111.6 0.3 fusion.1
  111.9 0.5 collective-permute-done.7
  112.4 0.5 multiply_reduce_fusion.5
  112.9 18.9 %all-reduce.15 = (f32[4]{0:T(128)S(1)}, f32[4]{0:T(128)S(1)}) all-reduce(f32[4]{0:T(128)S(1)} %get-tuple-element.10, f32[4]{0:T(128)S(1)} %get-tuple-element.9), channel_id=1, replica_groups=mesh['gx_0'=8,'gx_1'=2,'gy'=16,'gz'=4] {'gx_0'}, use_global_device_ids=true, to_apply=%region_5.6 | all-reduce | flops 8 | bytes 64 | tf_op jit(solution)/shard_map/psum | solution.py:40
  131.8 2.5 all-reduce.19
  134.2 27.0 %all-reduce.13 = (f32[4]{0:T(128)S(1)}, f32[4]{0:T(128)S(1)}) all-reduce(f32[4]{0:T(128)S(1)} %get-tuple-element.51, f32[4]{0:T(128)S(1)} %get-tuple-element.52), channel_id=1, replica_groups=mesh['gx_0'=8,'gx_1'=2,'gy'=16,'gz'=4] {'gy'}, use_global_device_ids=true, to_apply=%region_7.8 | all-reduce | flops 8 | bytes 64 | tf_op jit(solution)/shard_map/psum | solution.py:40
  161.2 8.0 %all-reduce.17 = (f32[4]{0:T(128)S(1)}, f32[4]{0:T(128)S(1)}) all-reduce(f32[4]{0:T(128)S(1)} %get-tuple-element.21, f32[4]{0:T(128)S(1)} %get-tuple-element.22), channel_id=1, replica_groups=mesh['gx_0'=8,'gx_1'=2,'gy'=16,'gz'=4] {'gz'}, use_global_device_ids=true, to_apply=%region_8.9 | all-reduce | flops 8 | bytes 64 | tf_op jit(solution)/shard_map/psum | solution.py:40
  169.2 0.3 multiply_reduce_fusion.1
  169.5 0.1 fusion.116
  169.6 0.3 fusion.84
  169.9 4.8 %collective-permute-start.16 = (f32[4,8,8,1]{3,1,2,0:T(8,128)S(1)}, f32[4,8,8,1]{3,1,2,0:T(8,128)S(1)}, u32[]{:S(2)}, u32[]{:S(2)}) collective-permute-start(f32[4,8,8,1]{3,1,2,0:T(8,128)S(1)} %get-tuple-element.59), channel_id=1, source_target_pairs={{1,0},{2,1},{3,2},{5,4},{6,5},{7,6},{9,8},{10,9},{11,10},{13,12},{... | collective-permute-start | bytes 3080 | tf_op jit(solution)/shard_map/ppermute | solution.py:28
  174.8 1.9 collective-permute-start.17
  176.7 0.3 fusion
  176.9 1.3 collective-permute-start.14
  178.2 4.5 %collective-permute-start.15 = (f32[4,8,1,128]{3,1,2,0:T(8,128)S(1)}, f32[4,8,1,128]{3,1,2,0:T(8,128)S(1)}, u32[]{:S(2)}, u32[]{:S(2)}) collective-permute-start(f32[4,8,1,128]{3,1,2,0:T(8,128)S(1)} %get-tuple-element.63), channel_id=1, source_target_pairs={{0,4},{4,8},{8,12},{12,16},{16,20},{20,24},{24,28},{28,32},{32,36}... | collective-permute-start | bytes 49160 | tf_op jit(solution)/shard_map/ppermute | solution.py:27
  182.8 1.3 collective-permute-start.12
  184.1 3.0 %collective-permute-start.13 = (f32[4,1,8,128]{3,1,2,0:T(1,128)S(1)}, f32[4,1,8,128]{3,1,2,0:T(1,128)S(1)}, u32[]{:S(2)}, u32[]{:S(2)}) collective-permute-start(f32[4,1,8,128]{3,1,2,0:T(1,128)S(1)} %get-tuple-element.61), channel_id=1, source_target_pairs={{0,64},{64,128},{128,192},{192,256},{256,320},{320,384},{384,448},... | collective-permute-start | bytes 49160 | tf_op jit(solution)/shard_map/ppermute | solution.py:27
  187.2 1.7 convolution_bitcast_fusion.4
  188.9 0.0 collective-permute-done.15
  189.0 0.5 fusion.11
  189.5 30.6 %all-reduce.14 = (f32[4]{0:T(128)S(1)}, f32[4]{0:T(128)S(1)}, f32[4,3,8]{2,1,0:T(4,128)S(1)}, f32[4,8,8]{2,1,0:T(8,128)S(1)}, f32[4]{0:T(128)S(1)}, /*index=5*/f32[4]{0:T(128)S(1)}, f32[4]{0:T(128)S(1)}, f32[4]{0:T(128)S(1)}) all-reduce(f32[4]{0:T(128)S(1)} %get-tuple-element.7, ...), channel_id=1, replica_groups=mesh['gx_0'=8,'gx_1'=2,'gy'=16,'gz'=4] {'gx_0'}, use_global_device_ids=true, to_apply=%region_15.16 | all-reduce | flops 376 | bytes 3008 | tf_op jit(solution)/shard_map/psum | solution.py:40
  220.1 3.4 %all-reduce.18 = (f32[4]{0:T(128)S(1)}, f32[4]{0:T(128)S(1)}, f32[4,3,8]{2,1,0:T(4,128)S(1)}, f32[4,8,8]{2,1,0:T(8,128)S(1)}, f32[4]{0:T(128)S(1)}, /*index=5*/f32[4]{0:T(128)S(1)}, f32[4]{0:T(128)S(1)}, f32[4]{0:T(128)S(1)}) all-reduce(f32[4]{0:T(128)S(1)} %get-tuple-element.23, ...), channel_id=1, replica_groups=mesh['gx_0'=8,'gx_1'=2,'gy'=16,'gz'=4] {'gx_1'}, use_global_device_ids=true, to_apply=%region_16.17 | all-reduce | flops 376 | bytes 3008 | tf_op jit(solution)/shard_map/psum | solution.py:40
  223.5 54.5 %all-reduce.12 = (f32[4]{0:T(128)S(1)}, f32[4]{0:T(128)S(1)}, f32[4,3,8]{2,1,0:T(4,128)S(1)}, f32[4,8,8]{2,1,0:T(8,128)S(1)}, f32[4]{0:T(128)S(1)}, /*index=5*/f32[4]{0:T(128)S(1)}, f32[4]{0:T(128)S(1)}, f32[4]{0:T(128)S(1)}) all-reduce(f32[4]{0:T(128)S(1)} %get-tuple-element.43, ...), channel_id=1, replica_groups=mesh['gx_0'=8,'gx_1'=2,'gy'=16,'gz'=4] {'gy'}, use_global_device_ids=true, to_apply=%region_17.18 | all-reduce | flops 376 | bytes 3008 | tf_op jit(solution)/shard_map/psum | solution.py:40
  278.0 15.7 %all-reduce.16 = (f32[4]{0:T(128)S(1)}, f32[4]{0:T(128)S(1)}, f32[4,3,8]{2,1,0:T(4,128)S(1)}, f32[4,8,8]{2,1,0:T(8,128)S(1)}, f32[4]{0:T(128)S(1)}, /*index=5*/f32[4]{0:T(128)S(1)}, f32[4]{0:T(128)S(1)}, f32[4]{0:T(128)S(1)}) all-reduce(f32[4]{0:T(128)S(1)} %get-tuple-element.13, ...), channel_id=1, replica_groups=mesh['gx_0'=8,'gx_1'=2,'gy'=16,'gz'=4] {'gz'}, use_global_device_ids=true, to_apply=%region_18.19 | all-reduce | flops 376 | bytes 3008 | tf_op jit(solution)/shard_map/psum | solution.py:40
  293.8 0.1 add_multiply_fusion
  293.9 0.2 fusion.101
  294.0 0.2 multiply_reduce_fusion.8
  294.2 0.7 fusion.15
  294.9 0.1 fusion.83
  295.0 0.7 copy.23
  295.7 0.6 copy.24
  (47 shorter events, 0.3 us)
Async XLA Ops:
  0.6 88.9 %copy-start = (f32[8,8]{1,0:T(8,128)S(1)}, f32[8,8]{1,0:T(8,128)}, u32[]{:S(2)}) copy-start(f32[8,8]{1,0:T(8,128)} %param.9) | copy-start | bytes 772
  0.6 74.4 %copy-start.1 = (bf16[4,8,8,8,128]{4,3,2,1,0:T(8,128)(2,1)S(1)}, bf16[4,8,8,8,128]{4,3,2,1,0:T(8,128)(2,1)}, u32[]{:S(2)}) copy-start(bf16[4,8,8,8,128]{4,3,2,1,0:T(8,128)(2,1)} %param.6) | copy-start | bytes 1572868
  75.9 18.1 %collective-permute-start.4 = (f32[4,8,8,1]{3,1,2,0:T(8,128)S(1)}, f32[4,8,8,1]{3,1,2,0:T(8,128)S(1)}, u32[]{:S(2)}, u32[]{:S(2)}) collective-permute-start(f32[4,8,8,1]{3,1,2,0:T(8,128)S(1)} %get-tuple-element.71), channel_id=1, source_target_pairs={{1,0},{2,1},{3,2},{5,4},{6,5},{7,6},{9,8},{10,9},{11,10},{13,12},{... | collective-permute-start | bytes 3080 | tf_op jit(solution)/shard_map/ppermute | solution.py:28
  78.6 15.4 %collective-permute-start.5 = (f32[4,8,8,1]{3,1,2,0:T(8,128)S(1)}, f32[4,8,8,1]{3,1,2,0:T(8,128)S(1)}, u32[]{:S(2)}, u32[]{:S(2)}) collective-permute-start(f32[4,8,8,1]{3,1,2,0:T(8,128)S(1)} %get-tuple-element.72), channel_id=1, source_target_pairs={{0,1},{1,2},{2,3},{4,5},{5,6},{6,7},{8,9},{9,10},{10,11},{12,13},{... | collective-permute-start | bytes 3080 | tf_op jit(solution)/shard_map/ppermute | solution.py:27
  81.7 9.0 %collective-permute-start.2 = (f32[4,8,1,128]{3,1,2,0:T(8,128)S(1)}, f32[4,8,1,128]{3,1,2,0:T(8,128)S(1)}, u32[]{:S(2)}, u32[]{:S(2)}) collective-permute-start(f32[4,8,1,128]{3,1,2,0:T(8,128)S(1)} %get-tuple-element.76), channel_id=1, source_target_pairs={{4,0},{8,4},{12,8},{16,12},{20,16},{24,20},{28,24},{32,28},{36,32}... | collective-permute-start | bytes 49160 | tf_op jit(solution)/shard_map/ppermute | solution.py:28
  83.0 10.9 %collective-permute-start.3 = (f32[4,8,1,128]{3,1,2,0:T(8,128)S(1)}, f32[4,8,1,128]{3,1,2,0:T(8,128)S(1)}, u32[]{:S(2)}, u32[]{:S(2)}) collective-permute-start(f32[4,8,1,128]{3,1,2,0:T(8,128)S(1)} %get-tuple-element.75), channel_id=1, source_target_pairs={{0,4},{4,8},{8,12},{12,16},{16,20},{20,24},{24,28},{28,32},{32,36}... | collective-permute-start | bytes 49160 | tf_op jit(solution)/shard_map/ppermute | solution.py:27
  87.6 6.4 %collective-permute-start = (f32[4,1,8,128]{3,1,2,0:T(1,128)S(1)}, f32[4,1,8,128]{3,1,2,0:T(1,128)S(1)}, u32[]{:S(2)}, u32[]{:S(2)}) collective-permute-start(f32[4,1,8,128]{3,1,2,0:T(1,128)S(1)} %get-tuple-element.74), channel_id=1, source_target_pairs={{64,0},{128,64},{192,128},{256,192},{320,256},{384,320},{448,384},... | collective-permute-start | bytes 49160 | tf_op jit(solution)/shard_map/ppermute | solution.py:28
  90.3 3.6 %copy-start.2 = (f32[8,8,128]{2,1,0:T(8,128)S(1)}, f32[8,8,128]{2,1,0:T(8,128)}, u32[]{:S(2)}) copy-start(f32[8,8,128]{2,1,0:T(8,128)} %param.7) | copy-start | bytes 98308
  90.7 4.0 %copy-start.3 = (f32[4,8,8,128]{3,2,1,0:T(8,128)S(1)}, f32[4,8,8,128]{3,2,1,0:T(8,128)}, u32[]{:S(2)}) copy-start(f32[4,8,8,128]{3,2,1,0:T(8,128)} %param.5) | copy-start | bytes 393220
  90.7 4.0 %collective-permute-start.1 = (f32[4,1,8,128]{3,1,2,0:T(1,128)S(1)}, f32[4,1,8,128]{3,1,2,0:T(1,128)S(1)}, u32[]{:S(2)}, u32[]{:S(2)}) collective-permute-start(f32[4,1,8,128]{3,1,2,0:T(1,128)S(1)} %get-tuple-element.73), channel_id=1, source_target_pairs={{0,64},{64,128},{128,192},{192,256},{256,320},{320,384},{384,448},... | collective-permute-start | bytes 49160 | tf_op jit(solution)/shard_map/ppermute | solution.py:27
  94.0 0.8 copy-start.4
  95.5 13.0 %collective-permute-start.8 = (f32[4,8,1,128]{3,1,2,0:T(8,128)S(1)}, f32[4,8,1,128]{3,1,2,0:T(8,128)S(1)}, u32[]{:S(2)}, u32[]{:S(2)}) collective-permute-start(f32[4,8,1,128]{3,1,2,0:T(8,128)S(1)} %get-tuple-element.70), channel_id=1, source_target_pairs={{4,0},{8,4},{12,8},{16,12},{20,16},{24,20},{28,24},{32,28},{36,32}... | collective-permute-start | bytes 49160 | tf_op jit(solution)/shard_map/ppermute | solution.py:28
  96.8 15.1 %collective-permute-start.10 = (f32[4,8,8,1]{3,1,2,0:T(8,128)S(1)}, f32[4,8,8,1]{3,1,2,0:T(8,128)S(1)}, u32[]{:S(2)}, u32[]{:S(2)}) collective-permute-start(f32[4,8,8,1]{3,1,2,0:T(8,128)S(1)} %get-tuple-element.65), channel_id=1, source_target_pairs={{1,0},{2,1},{3,2},{5,4},{6,5},{7,6},{9,8},{10,9},{11,10},{13,12},{... | collective-permute-start | bytes 3080 | tf_op jit(solution)/shard_map/ppermute | solution.py:28
  99.9 12.0 %collective-permute-start.11 = (f32[4,8,8,1]{3,1,2,0:T(8,128)S(1)}, f32[4,8,8,1]{3,1,2,0:T(8,128)S(1)}, u32[]{:S(2)}, u32[]{:S(2)}) collective-permute-start(f32[4,8,8,1]{3,1,2,0:T(8,128)S(1)} %get-tuple-element.66), channel_id=1, source_target_pairs={{0,1},{1,2},{2,3},{4,5},{5,6},{6,7},{8,9},{9,10},{10,11},{12,13},{... | collective-permute-start | bytes 3080 | tf_op jit(solution)/shard_map/ppermute | solution.py:27
  102.7 9.2 %collective-permute-start.9 = (f32[4,8,1,128]{3,1,2,0:T(8,128)S(1)}, f32[4,8,1,128]{3,1,2,0:T(8,128)S(1)}, u32[]{:S(2)}, u32[]{:S(2)}) collective-permute-start(f32[4,8,1,128]{3,1,2,0:T(8,128)S(1)} %get-tuple-element.69), channel_id=1, source_target_pairs={{0,4},{4,8},{8,12},{12,16},{16,20},{20,24},{24,28},{28,32},{32,36}... | collective-permute-start | bytes 49160 | tf_op jit(solution)/shard_map/ppermute | solution.py:27
  107.3 4.7 %collective-permute-start.6 = (f32[4,1,8,128]{3,1,2,0:T(1,128)S(1)}, f32[4,1,8,128]{3,1,2,0:T(1,128)S(1)}, u32[]{:S(2)}, u32[]{:S(2)}) collective-permute-start(f32[4,1,8,128]{3,1,2,0:T(1,128)S(1)} %get-tuple-element.68), channel_id=1, source_target_pairs={{64,0},{128,64},{192,128},{256,192},{320,256},{384,320},{448,384},... | collective-permute-start | bytes 49160 | tf_op jit(solution)/shard_map/ppermute | solution.py:28
  108.6 3.9 %collective-permute-start.7 = (f32[4,1,8,128]{3,1,2,0:T(1,128)S(1)}, f32[4,1,8,128]{3,1,2,0:T(1,128)S(1)}, u32[]{:S(2)}, u32[]{:S(2)}) collective-permute-start(f32[4,1,8,128]{3,1,2,0:T(1,128)S(1)} %get-tuple-element.67), channel_id=1, source_target_pairs={{0,64},{64,128},{128,192},{192,256},{256,320},{320,384},{384,448},... | collective-permute-start | bytes 49160 | tf_op jit(solution)/shard_map/ppermute | solution.py:27
  169.9 19.1 %collective-permute-start.16 = (f32[4,8,8,1]{3,1,2,0:T(8,128)S(1)}, f32[4,8,8,1]{3,1,2,0:T(8,128)S(1)}, u32[]{:S(2)}, u32[]{:S(2)}) collective-permute-start(f32[4,8,8,1]{3,1,2,0:T(8,128)S(1)} %get-tuple-element.59), channel_id=1, source_target_pairs={{1,0},{2,1},{3,2},{5,4},{6,5},{7,6},{9,8},{10,9},{11,10},{13,12},{... | collective-permute-start | bytes 3080 | tf_op jit(solution)/shard_map/ppermute | solution.py:28
  174.8 14.2 %collective-permute-start.17 = (f32[4,8,8,1]{3,1,2,0:T(8,128)S(1)}, f32[4,8,8,1]{3,1,2,0:T(8,128)S(1)}, u32[]{:S(2)}, u32[]{:S(2)}) collective-permute-start(f32[4,8,8,1]{3,1,2,0:T(8,128)S(1)} %get-tuple-element.60), channel_id=1, source_target_pairs={{0,1},{1,2},{2,3},{4,5},{5,6},{6,7},{8,9},{9,10},{10,11},{12,13},{... | collective-permute-start | bytes 3080 | tf_op jit(solution)/shard_map/ppermute | solution.py:27
  176.9 7.2 %collective-permute-start.14 = (f32[4,8,1,128]{3,1,2,0:T(8,128)S(1)}, f32[4,8,1,128]{3,1,2,0:T(8,128)S(1)}, u32[]{:S(2)}, u32[]{:S(2)}) collective-permute-start(f32[4,8,1,128]{3,1,2,0:T(8,128)S(1)} %get-tuple-element.64), channel_id=1, source_target_pairs={{4,0},{8,4},{12,8},{16,12},{20,16},{24,20},{28,24},{32,28},{36,32}... | collective-permute-start | bytes 49160 | tf_op jit(solution)/shard_map/ppermute | solution.py:28
  178.2 10.7 %collective-permute-start.15 = (f32[4,8,1,128]{3,1,2,0:T(8,128)S(1)}, f32[4,8,1,128]{3,1,2,0:T(8,128)S(1)}, u32[]{:S(2)}, u32[]{:S(2)}) collective-permute-start(f32[4,8,1,128]{3,1,2,0:T(8,128)S(1)} %get-tuple-element.63), channel_id=1, source_target_pairs={{0,4},{4,8},{8,12},{12,16},{16,20},{20,24},{24,28},{28,32},{32,36}... | collective-permute-start | bytes 49160 | tf_op jit(solution)/shard_map/ppermute | solution.py:27
  182.8 6.2 %collective-permute-start.12 = (f32[4,1,8,128]{3,1,2,0:T(1,128)S(1)}, f32[4,1,8,128]{3,1,2,0:T(1,128)S(1)}, u32[]{:S(2)}, u32[]{:S(2)}) collective-permute-start(f32[4,1,8,128]{3,1,2,0:T(1,128)S(1)} %get-tuple-element.62), channel_id=1, source_target_pairs={{64,0},{128,64},{192,128},{256,192},{320,256},{384,320},{448,384},... | collective-permute-start | bytes 49160 | tf_op jit(solution)/shard_map/ppermute | solution.py:28
  184.1 4.9 %collective-permute-start.13 = (f32[4,1,8,128]{3,1,2,0:T(1,128)S(1)}, f32[4,1,8,128]{3,1,2,0:T(1,128)S(1)}, u32[]{:S(2)}, u32[]{:S(2)}) collective-permute-start(f32[4,1,8,128]{3,1,2,0:T(1,128)S(1)} %get-tuple-element.61), channel_id=1, source_target_pairs={{0,64},{64,128},{128,192},{192,256},{256,320},{320,384},{384,448},... | collective-permute-start | bytes 49160 | tf_op jit(solution)/shard_map/ppermute | solution.py:27
where the time goes:
time: 297 us; the launch traced here: 296 us
  blocking collectives  232 us (78%)
  starting transfers between devices  49.1 us (17%)
  matrix products  9.99 us (3%)
    psum x12, blocking collectives, by_axis(): return functools.reduce(lax.psum, axes, x)  232 us
    ppermute x9, starting transfers between devices, extended(): lax.ppermute(last, axis, up)  30.7 us
    ppermute x9, starting transfers between devices, extended(): lax.ppermute(leading, axis, [(b, a) for a, b in up])  18.4 us
  transfers between devices with their start and end apart: 18, of which 2 were waited for; matrix products, arithmetic and copies ran while one was open for 1% of the time, Pallas kernels for 0%

commit v1 on v0

v1 whole, which is shorter than its diff:
```python
import jax
import jax.numpy as jnp
from jax import lax
from jax.sharding import Mesh
from jax.sharding import PartitionSpec as P

GX = ("gx_0", "gx_1")
PLANE = ("gx_0", "gx_1", "gz")
LINE = ("gy",)

penalty = 0.15
epsilon = 1e-06
max_step = 10.0
highest = lax.Precision.HIGHEST


def total(values):
    shape = values.shape
    flat = values.reshape(-1)
    width = -(-flat.size // 128) * 128
    flat = jnp.pad(flat, (0, width - flat.size)).reshape(1, width)
    for axes in (PLANE, LINE):
        count = lax.axis_size(axes)
        copies = jnp.broadcast_to(flat[None], (count, 1, width))
        flat = lax.optimization_barrier(
            jnp.sum(lax.all_to_all(copies, axes, 0, 0), axis=0)
        )
    size = 1
    for extent in shape:
        size *= extent
    return flat.reshape(-1)[:size].reshape(shape)


def face(x, dim, last):
    length = x.shape[dim]
    return lax.slice_in_dim(x, length - 1 if last else 0, length if last else 1, axis=dim)


def upward(x, axis, dim):
    count = lax.axis_size(axis)
    return lax.ppermute(face(x, dim, True), axis, [(i, i + 1) for i in range(count - 1)])


def downward(x, axis, dim):
    count = lax.axis_size(axis)
    return lax.ppermute(face(x, dim, False), axis, [(i + 1, i) for i in range(count - 1)])


SIDES = (("gz", 3), ("gy", 2), (GX, 1))


def halo(x):
    return [(dim, upward(x, axis, dim), downward(x, axis, dim)) for axis, dim in SIDES]


def outer(x, faces):
    added = jnp.zeros_like(x)
    for dim, low, high in faces:
        position = lax.broadcasted_iota(jnp.int32, x.shape, dim)
        added = added + jnp.where(position == 0, low, 0.0)
        added = added + jnp.where(position == x.shape[dim] - 1, high, 0.0)
    return -penalty * added


def matrices(stiffness, size_z):
    points = stiffness.shape[0]
    row = lax.broadcasted_iota(jnp.int32, (points, points), 0)
    col = lax.broadcasted_iota(jnp.int32, (points, points), 1)
    ends = (row == col) & ((row == 0) | (row == points - 1))
    closed = stiffness + jnp.where(ends, penalty, 0.0)
    eye = jnp.where(row == col, 1.0, 0.0)
    plane = (closed[:, None, :, None] * eye[None, :, None, :]
             + eye[:, None, :, None] * closed[None, :, None, :]).reshape(points * points, points * points)
    row = lax.broadcasted_iota(jnp.int32, (size_z, size_z), 0)
    col = lax.broadcasted_iota(jnp.int32, (size_z, size_z), 1)
    spread_out = jnp.tile(closed, (size_z // points, size_z // points))
    line = jnp.where(row // points == col // points, spread_out, 0.0)
    edge = (jnp.abs(row - col) == 1) & (row // points != col // points)
    return plane, jnp.where(edge, -penalty, line)


def dots(a, b):
    return jnp.sum(a * b, axis=(1, 2, 3))


def per_solve(values):
    return values[:, None, None, None]


def on_device(rhs, basis, inertia, helm, stiffness):
    solves, size_x, size_y, size_z = rhs.shape
    point_count = float(rhs[0].size * lax.axis_size(PLANE + LINE))
    diagonal = helm[:, None, None, None] * inertia[None]
    plane, line = matrices(stiffness, size_z)

    def inner(v):
        flat = v.reshape(solves, size_x * size_y, size_z)
        along = jnp.einsum("ij,sjc->sic", plane, flat, precision=highest)
        along = along + jnp.einsum("sjc,cd->sjd", flat, line, precision=highest)
        return diagonal * v + along.reshape(v.shape)

    def combine(weights):
        return jnp.einsum("sk,skxyz->sxyz", weights, basis, precision=highest)

    coef = total(jnp.einsum("skxyz,sxyz->sk", basis, rhs, precision=highest)) / point_count
    start = combine(coef)
    resid = rhs - inner(start) - outer(start, halo(start))
    image = inner(resid) + outer(resid, halo(resid))

    lows = [upward(image, axis, dim) for axis, dim in SIDES]
    cubic = dots(image, inner(image))
    for (_, dim), low in zip(SIDES, lows):
        cubic = cubic - 2.0 * penalty * dots(face(image, dim, False), low)
    pair = jnp.stack([resid, image], axis=1)
    moment = jnp.einsum("skxyz,smxyz->smk", basis, pair, precision=highest)
    gram = jnp.einsum("skxyz,slxyz->skl", basis, basis, preferred_element_type=jnp.float32)
    powers = jnp.stack([dots(resid, resid), dots(resid, image), dots(image, image), cubic], axis=1)
    sums = total(jnp.concatenate(
        [powers, moment.reshape(solves, -1), gram.reshape(solves, -1)], axis=1)) / point_count
    keep = coef.shape[1]
    mu0, mu1, mu2, mu3 = (sums[:, i] for i in range(4))
    moment = sums[:, 4:4 + 2 * keep].reshape(solves, 2, keep)
    gram = sums[:, 4 + 2 * keep:].reshape(solves, keep, keep)

    step_0 = mu0 / mu1
    next_0 = jnp.maximum(step_0 * step_0 * mu2 - mu0, 0.0)
    ratio = next_0 / mu0
    grown = 1.0 + ratio
    curvature = grown * grown * mu1 - 2.0 * grown * step_0 * mu2 + step_0 * step_0 * mu3
    step_1 = jnp.where(curvature * max_step > next_0, next_0 / curvature, max_step)
    of_resid = step_0 + step_1 * grown
    of_image = -step_1 * step_0
    change = of_resid[:, None] * moment[:, 0] + of_image[:, None] * moment[:, 1]
    weights = jnp.einsum("skl,sl->sk", gram, coef, precision=highest) + change
    left = coef - weights
    spread = (
        jnp.einsum("sk,skl,sl->s", left, gram, left, precision=highest)
        + 2.0 * jnp.sum(left * change, axis=1)
        + of_resid * of_resid * mu0 + 2.0 * of_resid * of_image * mu1 + of_image * of_image * mu2
    )
    iterate = start + per_solve(of_resid) * resid + per_solve(of_image) * image
    remainder = iterate - combine(weights)
    new_basis = (remainder * per_solve(lax.rsqrt(spread + epsilon))).astype(jnp.bfloat16)
    return (iterate, new_basis)


def solution(mesh):
    torus = Mesh(
        mesh.devices.reshape(mesh.shape["gx"] // 2, 2, mesh.shape["gy"], mesh.shape["gz"]),
        ("gx_0", "gx_1", "gy", "gz"),
    )
    placed = (P(None, GX, "gy", "gz"), P(None, None, GX, "gy", "gz"), P(GX, "gy", "gz"), P(), P())
    return jax.shard_map(
        on_device,
        mesh=torus,
        in_specs=placed,
        out_specs=(P(None, GX, "gy", "gz"), P(None, GX, "gy", "gz")),
        check_vma=False,
    )
```

time: 297 us -> 151 us (0.51)
  the two profiles are of different devices: /device:TPU:4 before, /device:TPU:8 now
where the time goes in v1:
time: 151 us; the launch traced here: 150 us
  starting transfers between devices  77.4 us (51%)
  waiting for transfers between devices  34.4 us (23%)
  blocking collectives  18.7 us (12%)
  matrix products  8.18 us (5%)
  local copies, waits for them, and re-layouts  7.55 us (5%)
  other arithmetic  2.8 us (2%)
    all_to_all x3, starting transfers between devices, total(): lax.all_to_all(copies, axes, 0, 0)  35.9 us
    all_to_all x3, waiting for transfers between devices, total(): lax.all_to_all(copies, axes, 0, 0)  31.2 us
    ppermute x9, starting transfers between devices, upward(): lax.ppermute(face(x, dim, True), axis, [(i, i + 1) for i in range(count -...  29.2 us
    all_to_all x1, blocking collectives, total(): lax.all_to_all(copies, axes, 0, 0)  18.7 us
    ppermute x6, starting transfers between devices, downward(): lax.ppermute(face(x, dim, False), axis, [(i + 1, i) for i in range(count...  12.3 us
  transfers between devices with their start and end apart: 18, of which 6 were waited for; matrix products, arithmetic and copies ran while one was open for 3% of the time, Pallas kernels for 0%

profile of v1, /device:TPU:8, one launch (start us, length us, event | category | flops | bytes accessed | tf_op | source)
XLA Modules:
  0.0 150.2 jit_solution(740846932756025444)
XLA Ops:
  0.6 2.6 %fusion.9 = f32[4,1,8,1,1]{2,1,4,3,0:T(1,128)S(1)} fusion(f32[4,8,8,128,1]{3,4,2,1,0:T(1,128)} %bitcast.124, bf16[4,8,8,8,128]{4,3,2,1,0:T(8,128)(2,1)} %param.6), kind=kOutput, calls=%fused_computation.21 | convolution fusion | flops 3145728 | bytes 655488 | tf_op jit(solution)/shard_map/skxyz,sxyz->sk/dot_general | solution.py:105
  3.4 0.6 broadcast_in_dim.169
  4.0 17.1 %all-to-all-start = ((f32[64,1,128]{2,1,0:T(1,128)}), f32[64,1,128]{2,1,0:T(1,128)S(1)}, u32[]{:S(2)}, u32[]{:S(2)}) async-start(f32[64,1,128]{2,1,0:T(1,128)} %broadcast_in_dim.169), calls=%async_computation | async-start | bytes 65536 | tf_op jit(solution)/shard_map/all_to_all | solution.py:26
  21.2 0.5 convolution_bitcast_fusion.3
  21.8 0.1 copy-done.4
  22.1 0.6 select_select_fusion
  22.7 7.1 %all-to-all-done = f32[64,1,128]{2,1,0:T(1,128)S(1)} async-done(((f32[64,1,128]{2,1,0:T(1,128)}), f32[64,1,128]{2,1,0:T(1,128)S(1)}, u32[]{:S(2)}, u32[]{:S(2)}) %all-to-all-start) | async-done | bytes 32800 | tf_op jit(solution)/shard_map/all_to_all | solution.py:26
  29.9 0.6 broadcast_in_dim.171
  30.5 12.2 %all-to-all-start.1 = ((f32[16,1,128]{2,1,0:T(1,128)}), f32[16,1,128]{2,1,0:T(1,128)S(1)}, u32[]{:S(2)}, u32[]{:S(2)}) async-start(f32[16,1,128]{2,1,0:T(1,128)} %broadcast_in_dim.171), calls=%async_computation.1 | async-start | bytes 16384 | tf_op jit(solution)/shard_map/all_to_all | solution.py:26
  42.7 0.1 reshape.782
  42.9 0.5 reshape.783
  43.5 11.7 %all-to-all-done.1 = f32[16,1,128]{2,1,0:T(1,128)S(1)} async-done(((f32[16,1,128]{2,1,0:T(1,128)}), f32[16,1,128]{2,1,0:T(1,128)S(1)}, u32[]{:S(2)}, u32[]{:S(2)}) %all-to-all-start.1) | async-done | bytes 8224 | tf_op jit(solution)/shard_map/all_to_all | solution.py:26
  55.2 0.7 fusion.7
  56.1 2.5 %collective-permute-start = (f32[4,8,8,1]{3,2,0,1:T(8,128)S(1)}, f32[4,8,8,1]{3,2,0,1:T(8,128)S(1)}, u32[]{:S(2)}, u32[]{:S(2)}) collective-permute-start(f32[4,8,8,1]{3,2,0,1:T(8,128)S(1)} %get-tuple-element.40), channel_id=1, source_target_pairs={{0,1},{1,2},{2,3},{4,5},{5,6},{6,7},{8,9},{9,10},{10,11},{12,13},{... | collective-permute-start | bytes 3080 | tf_op jit(solution)/shard_map/ppermute | solution.py:41
  58.6 1.3 collective-permute-start.1
  59.9 2.5 %collective-permute-start.2 = (f32[4,8,1,128]{3,2,0,1:T(1,128)S(1)}, f32[4,8,1,128]{3,2,0,1:T(1,128)S(1)}, u32[]{:S(2)}, u32[]{:S(2)}) collective-permute-start(f32[4,8,1,128]{3,2,0,1:T(1,128)S(1)} %get-tuple-element.42), channel_id=1, source_target_pairs={{0,4},{4,8},{8,12},{12,16},{16,20},{20,24},{24,28},{28,32},{32,36}... | collective-permute-start | bytes 49160 | tf_op jit(solution)/shard_map/ppermute | solution.py:41
  62.4 1.3 collective-permute-start.3
  63.7 1.9 %collective-permute-start.4 = (f32[4,1,8,128]{3,2,0,1:T(8,128)S(1)}, f32[4,1,8,128]{3,2,0,1:T(8,128)S(1)}, u32[]{:S(2)}, u32[]{:S(2)}) collective-permute-start(f32[4,1,8,128]{3,2,0,1:T(8,128)S(1)} %get-tuple-element.44), channel_id=1, source_target_pairs={{0,64},{64,128},{128,192},{192,256},{256,320},{320,384},{384,448},... | collective-permute-start | bytes 49160 | tf_op jit(solution)/shard_map/ppermute | solution.py:41
  65.7 0.3 convolution_bitcast_fusion.2
  65.9 3.6 %collective-permute-start.5 = (f32[4,1,8,128]{3,2,0,1:T(8,128)S(1)}, f32[4,1,8,128]{3,2,0,1:T(8,128)S(1)}, u32[]{:S(2)}, u32[]{:S(2)}) collective-permute-start(f32[4,1,8,128]{3,2,0,1:T(8,128)S(1)} %get-tuple-element.45), channel_id=1, source_target_pairs={{64,0},{128,64},{192,128},{256,192},{320,256},{384,320},{448,384},... | collective-permute-start | bytes 49160 | tf_op jit(solution)/shard_map/ppermute | solution.py:46
  69.6 0.3 fusion.2
  69.9 0.2 copy.101
  70.1 0.2 copy.103
  70.4 0.6 collective-permute-done.5
  71.0 0.1 copy-done.1
  71.2 0.5 copy-done.3
  71.7 0.2 fusion.17
  71.9 0.3 convolution_bitcast_fusion.1
  72.3 4.6 %collective-permute-start.6 = (f32[4,8,8,1]{3,2,0,1:T(8,128)S(1)}, f32[4,8,8,1]{3,2,0,1:T(8,128)S(1)}, u32[]{:S(2)}, u32[]{:S(2)}) collective-permute-start(f32[4,8,8,1]{3,2,0,1:T(8,128)S(1)} %get-tuple-element.34), channel_id=1, source_target_pairs={{0,1},{1,2},{2,3},{4,5},{5,6},{6,7},{8,9},{9,10},{10,11},{12,13},{... | collective-permute-start | bytes 3080 | tf_op jit(solution)/shard_map/ppermute | solution.py:41
  76.8 1.3 collective-permute-start.7
  78.1 4.5 %collective-permute-start.8 = (f32[4,8,1,128]{3,2,0,1:T(1,128)S(1)}, f32[4,8,1,128]{3,2,0,1:T(1,128)S(1)}, u32[]{:S(2)}, u32[]{:S(2)}) collective-permute-start(f32[4,8,1,128]{3,2,0,1:T(1,128)S(1)} %get-tuple-element.36), channel_id=1, source_target_pairs={{0,4},{4,8},{8,12},{12,16},{16,20},{20,24},{24,28},{28,32},{32,36}... | collective-permute-start | bytes 49160 | tf_op jit(solution)/shard_map/ppermute | solution.py:41
  82.7 1.3 collective-permute-start.9
  84.0 2.0 %collective-permute-start.10 = (f32[4,1,8,128]{3,2,0,1:T(8,128)S(1)}, f32[4,1,8,128]{3,2,0,1:T(8,128)S(1)}, u32[]{:S(2)}, u32[]{:S(2)}) collective-permute-start(f32[4,1,8,128]{3,2,0,1:T(8,128)S(1)} %get-tuple-element.38), channel_id=1, source_target_pairs={{0,64},{64,128},{128,192},{192,256},{256,320},{320,384},{384,448},... | collective-permute-start | bytes 49160 | tf_op jit(solution)/shard_map/ppermute | solution.py:41
  86.0 3.5 %collective-permute-start.11 = (f32[4,1,8,128]{3,2,0,1:T(8,128)S(1)}, f32[4,1,8,128]{3,2,0,1:T(8,128)S(1)}, u32[]{:S(2)}, u32[]{:S(2)}) collective-permute-start(f32[4,1,8,128]{3,2,0,1:T(8,128)S(1)} %get-tuple-element.39), channel_id=1, source_target_pairs={{64,0},{128,64},{192,128},{256,192},{320,256},{384,320},{448,384},... | collective-permute-start | bytes 49160 | tf_op jit(solution)/shard_map/ppermute | solution.py:46
  89.6 0.3 fusion.1
  89.8 0.2 copy.107
  90.1 0.3 copy.109
  90.4 0.6 collective-permute-done.11
  91.0 0.2 fusion.19
  91.3 0.3 convolution_bitcast_fusion
  91.6 1.7 %convolution_bitcast_fusion.4 = f32[4,2,8]{2,1,0:T(2,128)S(1)} fusion(bf16[4,8,8,8,128]{4,3,2,1,0:T(8,128)(2,1)S(1)} %copy-done, f32[4,1,8,8,128]{4,1,3,0,2:T(1,128)S(1)} %bitcast.117, f32[4,1,8,8,128]{4,1,3,0,2:T(1,128)S(1)} %bitcast.116), kind=kOutput, calls=%fused_computation.12 | convolution fusion | flops 6356992 | bytes 786688 | tf_op jit(solution)/shard_map/skxyz,smxyz->smk/dot_general | solution.py:115
  93.4 4.6 %collective-permute-start.12 = (f32[4,8,8,1]{3,2,0,1:T(8,128)S(1)}, f32[4,8,8,1]{3,2,0,1:T(8,128)S(1)}, u32[]{:S(2)}, u32[]{:S(2)}) collective-permute-start(f32[4,8,8,1]{3,2,0,1:T(8,128)S(1)} %slice.127), channel_id=1, source_target_pairs={{0,1},{1,2},{2,3},{4,5},{5,6},{6,7},{8,9},{9,10},{10,11},{12,13},{... | collective-permute-start | bytes 3080 | tf_op jit(solution)/shard_map/ppermute | solution.py:41
  97.9 4.5 %collective-permute-start.13 = (f32[4,8,1,128]{3,2,0,1:T(1,128)S(1)}, f32[4,8,1,128]{3,2,0,1:T(1,128)S(1)}, u32[]{:S(2)}, u32[]{:S(2)}) collective-permute-start(f32[4,8,1,128]{3,2,0,1:T(1,128)S(1)} %slice.129), channel_id=1, source_target_pairs={{0,4},{4,8},{8,12},{12,16},{16,20},{20,24},{24,28},{28,32},{32,36}... | collective-permute-start | bytes 49160 | tf_op jit(solution)/shard_map/ppermute | solution.py:41
  102.5 2.1 %collective-permute-start.14 = (f32[4,1,8,128]{3,2,0,1:T(8,128)S(1)}, f32[4,1,8,128]{3,2,0,1:T(8,128)S(1)}, u32[]{:S(2)}, u32[]{:S(2)}) collective-permute-start(f32[4,1,8,128]{3,2,0,1:T(8,128)S(1)} %slice.131), channel_id=1, source_target_pairs={{0,64},{64,128},{128,192},{192,256},{256,320},{320,384},{384,448},... | collective-permute-start | bytes 49160 | tf_op jit(solution)/shard_map/ppermute | solution.py:41
  104.6 0.3 fusion
  104.8 0.2 fusion.22
  105.3 0.1 fusion.23
  105.4 0.1 fusion.35
  105.6 2.0 %collective-permute-done.14 = f32[4,1,8,128]{3,2,0,1:T(8,128)S(1)} collective-permute-done((f32[4,1,8,128]{3,2,0,1:T(8,128)S(1)}, f32[4,1,8,128]{3,2,0,1:T(8,128)S(1)}, u32[]{:S(2)}, u32[]{:S(2)}) %collective-permute-start.14) | collective-permute-done | bytes 16416 | tf_op jit(solution)/shard_map/ppermute | solution.py:41
  107.6 0.1 fusion.34
  107.8 0.1 concatenate.3
  108.0 18.7 %all_to_all.20 = f32[64,1,384]{2,1,0:T(1,128)S(1)} all-to-all(f32[64,1,384]{2,1,0:T(1,128)S(1)} %broadcast_in_dim.202), channel_id=1, replica_groups=mesh['gx_0'=8,'gx_1'=2,'gy'=16,'gz'=4] {'gx_0','gx_1','gz'}, dimensions={0} | all-to-all | bytes 196608 | tf_op jit(solution)/shard_map/all_to_all | solution.py:26
  126.7 0.1 reduce_sum.127
  126.9 0.6 broadcast_in_dim.204
  127.5 6.5 %all-to-all-start.3 = ((f32[16,1,384]{2,1,0:T(1,128)}), f32[16,1,384]{2,1,0:T(1,128)S(1)}, u32[]{:S(2)}, u32[]{:S(2)}) async-start(f32[16,1,384]{2,1,0:T(1,128)} %broadcast_in_dim.204), calls=%async_computation.3 | async-start | bytes 49152 | tf_op jit(solution)/shard_map/all_to_all | solution.py:26
  134.2 12.4 %all-to-all-done.3 = f32[16,1,384]{2,1,0:T(1,128)S(1)} async-done(((f32[16,1,384]{2,1,0:T(1,128)}), f32[16,1,384]{2,1,0:T(1,128)S(1)}, u32[]{:S(2)}, u32[]{:S(2)}) %all-to-all-start.3) | async-done | bytes 24608 | tf_op jit(solution)/shard_map/all_to_all | solution.py:26
  147.1 0.3 add_reduce_fusion
  147.4 0.2 fusion.55
  147.6 0.2 fusion.56
  147.8 0.2 multiply_reduce_fusion.4
  148.0 0.7 fusion.5
  148.8 0.1 fusion.25
  148.9 0.7 copy.123
  149.6 0.6 copy.124
  (74 shorter events, 2.5 us)
Async XLA Ops:
  0.6 20.6 %copy-start = (bf16[4,8,8,8,128]{4,3,2,1,0:T(8,128)(2,1)S(1)}, bf16[4,8,8,8,128]{4,3,2,1,0:T(8,128)(2,1)}, u32[]{:S(2)}) copy-start(bf16[4,8,8,8,128]{4,3,2,1,0:T(8,128)(2,1)} %param.6) | copy-start | bytes 1572868
  4.0 25.9 %all-to-all-start = ((f32[64,1,128]{2,1,0:T(1,128)}), f32[64,1,128]{2,1,0:T(1,128)S(1)}, u32[]{:S(2)}, u32[]{:S(2)}) async-start(f32[64,1,128]{2,1,0:T(1,128)} %broadcast_in_dim.169), calls=%async_computation | async-start | bytes 65536 | tf_op jit(solution)/shard_map/all_to_all | solution.py:26
  21.2 0.7 copy-start.4
  30.5 24.6 %all-to-all-start.1 = ((f32[16,1,128]{2,1,0:T(1,128)}), f32[16,1,128]{2,1,0:T(1,128)S(1)}, u32[]{:S(2)}, u32[]{:S(2)}) async-start(f32[16,1,128]{2,1,0:T(1,128)} %broadcast_in_dim.171), calls=%async_computation.1 | async-start | bytes 16384 | tf_op jit(solution)/shard_map/all_to_all | solution.py:26
  56.1 9.8 %collective-permute-start = (f32[4,8,8,1]{3,2,0,1:T(8,128)S(1)}, f32[4,8,8,1]{3,2,0,1:T(8,128)S(1)}, u32[]{:S(2)}, u32[]{:S(2)}) collective-permute-start(f32[4,8,8,1]{3,2,0,1:T(8,128)S(1)} %get-tuple-element.40), channel_id=1, source_target_pairs={{0,1},{1,2},{2,3},{4,5},{5,6},{6,7},{8,9},{9,10},{10,11},{12,13},{... | collective-permute-start | bytes 3080 | tf_op jit(solution)/shard_map/ppermute | solution.py:41
  58.6 11.5 %collective-permute-start.1 = (f32[4,8,8,1]{3,2,0,1:T(8,128)S(1)}, f32[4,8,8,1]{3,2,0,1:T(8,128)S(1)}, u32[]{:S(2)}, u32[]{:S(2)}) collective-permute-start(f32[4,8,8,1]{3,2,0,1:T(8,128)S(1)} %get-tuple-element.41), channel_id=1, source_target_pairs={{1,0},{2,1},{3,2},{5,4},{6,5},{7,6},{9,8},{10,9},{11,10},{13,12},{... | collective-permute-start | bytes 3080 | tf_op jit(solution)/shard_map/ppermute | solution.py:46
  59.9 10.5 %collective-permute-start.2 = (f32[4,8,1,128]{3,2,0,1:T(1,128)S(1)}, f32[4,8,1,128]{3,2,0,1:T(1,128)S(1)}, u32[]{:S(2)}, u32[]{:S(2)}) collective-permute-start(f32[4,8,1,128]{3,2,0,1:T(1,128)S(1)} %get-tuple-element.42), channel_id=1, source_target_pairs={{0,4},{4,8},{8,12},{12,16},{16,20},{20,24},{24,28},{28,32},{32,36}... | collective-permute-start | bytes 49160 | tf_op jit(solution)/shard_map/ppermute | solution.py:41
  62.4 8.0 %collective-permute-start.3 = (f32[4,8,1,128]{3,2,0,1:T(1,128)S(1)}, f32[4,8,1,128]{3,2,0,1:T(1,128)S(1)}, u32[]{:S(2)}, u32[]{:S(2)}) collective-permute-start(f32[4,8,1,128]{3,2,0,1:T(1,128)S(1)} %get-tuple-element.43), channel_id=1, source_target_pairs={{4,0},{8,4},{12,8},{16,12},{20,16},{24,20},{28,24},{32,28},{36,32}... | collective-permute-start | bytes 49160 | tf_op jit(solution)/shard_map/ppermute | solution.py:46
  63.7 6.7 %collective-permute-start.4 = (f32[4,1,8,128]{3,2,0,1:T(8,128)S(1)}, f32[4,1,8,128]{3,2,0,1:T(8,128)S(1)}, u32[]{:S(2)}, u32[]{:S(2)}) collective-permute-start(f32[4,1,8,128]{3,2,0,1:T(8,128)S(1)} %get-tuple-element.44), channel_id=1, source_target_pairs={{0,64},{64,128},{128,192},{192,256},{256,320},{320,384},{384,448},... | collective-permute-start | bytes 49160 | tf_op jit(solution)/shard_map/ppermute | solution.py:41
  65.9 5.1 %collective-permute-start.5 = (f32[4,1,8,128]{3,2,0,1:T(8,128)S(1)}, f32[4,1,8,128]{3,2,0,1:T(8,128)S(1)}, u32[]{:S(2)}, u32[]{:S(2)}) collective-permute-start(f32[4,1,8,128]{3,2,0,1:T(8,128)S(1)} %get-tuple-element.45), channel_id=1, source_target_pairs={{64,0},{128,64},{192,128},{256,192},{320,256},{384,320},{448,384},... | collective-permute-start | bytes 49160 | tf_op jit(solution)/shard_map/ppermute | solution.py:46
  70.1 0.9 copy-start.2
  70.4 0.8 copy-start.1
  71.0 0.7 copy-start.3
  72.3 13.8 %collective-permute-start.6 = (f32[4,8,8,1]{3,2,0,1:T(8,128)S(1)}, f32[4,8,8,1]{3,2,0,1:T(8,128)S(1)}, u32[]{:S(2)}, u32[]{:S(2)}) collective-permute-start(f32[4,8,8,1]{3,2,0,1:T(8,128)S(1)} %get-tuple-element.34), channel_id=1, source_target_pairs={{0,1},{1,2},{2,3},{4,5},{5,6},{6,7},{8,9},{9,10},{10,11},{12,13},{... | collective-permute-start | bytes 3080 | tf_op jit(solution)/shard_map/ppermute | solution.py:41
  76.8 13.3 %collective-permute-start.7 = (f32[4,8,8,1]{3,2,0,1:T(8,128)S(1)}, f32[4,8,8,1]{3,2,0,1:T(8,128)S(1)}, u32[]{:S(2)}, u32[]{:S(2)}) collective-permute-start(f32[4,8,8,1]{3,2,0,1:T(8,128)S(1)} %get-tuple-element.35), channel_id=1, source_target_pairs={{1,0},{2,1},{3,2},{5,4},{6,5},{7,6},{9,8},{10,9},{11,10},{13,12},{... | collective-permute-start | bytes 3080 | tf_op jit(solution)/shard_map/ppermute | solution.py:46
  78.1 12.3 %collective-permute-start.8 = (f32[4,8,1,128]{3,2,0,1:T(1,128)S(1)}, f32[4,8,1,128]{3,2,0,1:T(1,128)S(1)}, u32[]{:S(2)}, u32[]{:S(2)}) collective-permute-start(f32[4,8,1,128]{3,2,0,1:T(1,128)S(1)} %get-tuple-element.36), channel_id=1, source_target_pairs={{0,4},{4,8},{8,12},{12,16},{16,20},{20,24},{24,28},{28,32},{32,36}... | collective-permute-start | bytes 49160 | tf_op jit(solution)/shard_map/ppermute | solution.py:41
  82.7 7.7 %collective-permute-start.9 = (f32[4,8,1,128]{3,2,0,1:T(1,128)S(1)}, f32[4,8,1,128]{3,2,0,1:T(1,128)S(1)}, u32[]{:S(2)}, u32[]{:S(2)}) collective-permute-start(f32[4,8,1,128]{3,2,0,1:T(1,128)S(1)} %get-tuple-element.37), channel_id=1, source_target_pairs={{4,0},{8,4},{12,8},{16,12},{20,16},{24,20},{28,24},{32,28},{36,32}... | collective-permute-start | bytes 49160 | tf_op jit(solution)/shard_map/ppermute | solution.py:46
  84.0 6.4 %collective-permute-start.10 = (f32[4,1,8,128]{3,2,0,1:T(8,128)S(1)}, f32[4,1,8,128]{3,2,0,1:T(8,128)S(1)}, u32[]{:S(2)}, u32[]{:S(2)}) collective-permute-start(f32[4,1,8,128]{3,2,0,1:T(8,128)S(1)} %get-tuple-element.38), channel_id=1, source_target_pairs={{0,64},{64,128},{128,192},{192,256},{256,320},{320,384},{384,448},... | collective-permute-start | bytes 49160 | tf_op jit(solution)/shard_map/ppermute | solution.py:41
  86.0 4.9 %collective-permute-start.11 = (f32[4,1,8,128]{3,2,0,1:T(8,128)S(1)}, f32[4,1,8,128]{3,2,0,1:T(8,128)S(1)}, u32[]{:S(2)}, u32[]{:S(2)}) collective-permute-start(f32[4,1,8,128]{3,2,0,1:T(8,128)S(1)} %get-tuple-element.39), channel_id=1, source_target_pairs={{64,0},{128,64},{192,128},{256,192},{320,256},{384,320},{448,384},... | collective-permute-start | bytes 49160 | tf_op jit(solution)/shard_map/ppermute | solution.py:46
  93.4 11.9 %collective-permute-start.12 = (f32[4,8,8,1]{3,2,0,1:T(8,128)S(1)}, f32[4,8,8,1]{3,2,0,1:T(8,128)S(1)}, u32[]{:S(2)}, u32[]{:S(2)}) collective-permute-start(f32[4,8,8,1]{3,2,0,1:T(8,128)S(1)} %slice.127), channel_id=1, source_target_pairs={{0,1},{1,2},{2,3},{4,5},{5,6},{6,7},{8,9},{9,10},{10,11},{12,13},{... | collective-permute-start | bytes 3080 | tf_op jit(solution)/shard_map/ppermute | solution.py:41
  97.9 7.5 %collective-permute-start.13 = (f32[4,8,1,128]{3,2,0,1:T(1,128)S(1)}, f32[4,8,1,128]{3,2,0,1:T(1,128)S(1)}, u32[]{:S(2)}, u32[]{:S(2)}) collective-permute-start(f32[4,8,1,128]{3,2,0,1:T(1,128)S(1)} %slice.129), channel_id=1, source_target_pairs={{0,4},{4,8},{8,12},{12,16},{16,20},{20,24},{24,28},{28,32},{32,36}... | collective-permute-start | bytes 49160 | tf_op jit(solution)/shard_map/ppermute | solution.py:41
  102.5 5.1 %collective-permute-start.14 = (f32[4,1,8,128]{3,2,0,1:T(8,128)S(1)}, f32[4,1,8,128]{3,2,0,1:T(8,128)S(1)}, u32[]{:S(2)}, u32[]{:S(2)}) collective-permute-start(f32[4,1,8,128]{3,2,0,1:T(8,128)S(1)} %slice.131), channel_id=1, source_target_pairs={{0,64},{64,128},{128,192},{192,256},{256,320},{320,384},{384,448},... | collective-permute-start | bytes 49160 | tf_op jit(solution)/shard_map/ppermute | solution.py:41
  127.5 19.1 %all-to-all-start.3 = ((f32[16,1,384]{2,1,0:T(1,128)}), f32[16,1,384]{2,1,0:T(1,128)S(1)}, u32[]{:S(2)}, u32[]{:S(2)}) async-start(f32[16,1,384]{2,1,0:T(1,128)} %broadcast_in_dim.204), calls=%async_computation.3 | async-start | bytes 49152 | tf_op jit(solution)/shard_map/all_to_all | solution.py:26

commit v2 on v1

v2 whole, which is shorter than its diff:
```python
import jax
import jax.numpy as jnp
from jax import lax
from jax.experimental import pallas as pl
from jax.experimental.pallas import tpu as pltpu
from jax.sharding import Mesh
from jax.sharding import PartitionSpec as P

GX = ("gx_0", "gx_1")
PLANE = ("gx_0", "gx_1", "gz")
LINE = ("gy",)

penalty = 0.15
epsilon = 1e-06
max_step = 10.0
f32 = jnp.float32
S, K, X, Y, Z = 4, 8, 8, 8, 128
SX, SK, SXY = S * X, S * K, S * X * Y
DIAGONALS = 5
ROWS = 2 * SK + 16 + DIAGONALS * SK


def mm(a, b, left=1, right=0):
    return lax.dot_general(
        a, b, (((left,), (right,)), ((), ())), precision=lax.Precision.HIGHEST, preferred_element_type=f32
    )


def iota(shape, dim):
    return lax.broadcasted_iota(jnp.int32, shape, dim)


def where(mask):
    return jnp.where(mask, 1.0, 0.0).astype(f32)


def ends():
    row, col = iota((8, Z), 0), iota((8, Z), 1)
    return where(((row == 0) & (col == 0)) | ((row == 1) & (col == Z - 1)))


def stack_rows(first, second):
    row = iota((8, first.shape[1]), 0)
    return jnp.where(row == 0, first, jnp.where(row == 1, second, 0.0))


def spread(first, second):
    return mm(stack_rows(first, second), ends(), 0, 0)


def laplace(v, inertia, helm_ref, plane, line):
    along = mm(v, line)
    parts = []
    for s in range(S):
        part = v[s * X * Y:(s + 1) * X * Y]
        parts.append(helm_ref[s] * inertia * part + mm(plane, part))
    return along + jnp.concatenate(parts, axis=0)


def at_x(low, high):
    x = iota((S, X, Y, Z), 1)
    return jnp.where(x == 0, low[:, None], jnp.where(x == X - 1, high[:, None], 0.0))


def at_y(low, high):
    y = iota((S, X, Y, Z), 2)
    low, high = low.reshape(S, X, 1, Z), high.reshape(S, X, 1, Z)
    return jnp.where(y == 0, low, jnp.where(y == Y - 1, high, 0.0))


def column(values, at):
    return values[:, at:at + 1]


def weighted(weights, basis_ref, s):
    out = None
    for k in range(K):
        term = column(weights, s * K + k) * basis_ref[s, k].astype(f32).reshape(X * Y, Z)
        out = term if out is None else out + term
    return out


def row_sum(product):
    return jnp.sum(product.reshape(X * Y, Z), axis=0, keepdims=True)


def lane_sums(rows):
    return mm(jnp.ones((8, Z), f32), rows, 1, 1)[0:1]


def coef_kernel(rhs_ref, basis_ref, out_ref):
    rows = []
    for s in range(S):
        right = rhs_ref[s]
        for k in range(K):
            rows.append(row_sum(basis_ref[s, k].astype(f32) * right))
    rows = jnp.concatenate(rows + [jnp.zeros((Z - SK, Z), f32)], axis=0)
    out_ref[...] = jnp.broadcast_to(lane_sums(rows)[None], out_ref.shape)


def fold_kernel(in_ref, out_ref):
    out_ref[...] = jnp.broadcast_to(jnp.sum(in_ref[...], axis=0, keepdims=True), out_ref.shape)


def build(stiffness):
    row, col = iota((8, 8), 0), iota((8, 8), 1)
    closed = stiffness + jnp.where((row == col) & ((row == 0) | (row == 7)), penalty, 0.0)
    low = where(iota((X * Y, 8), 0) % 8 == iota((X * Y, 8), 1))
    high = where(iota((X * Y, 8), 0) // 8 == iota((X * Y, 8), 1))
    row, col = iota((X * Y, X * Y), 0), iota((X * Y, X * Y), 1)
    along_x = mm(mm(high, closed), high, 1, 1) * where(row % 8 == col % 8)
    along_y = mm(mm(low, closed), low, 1, 1) * where(row // 8 == col // 8)
    low = where(iota((Z, 8), 0) % 8 == iota((Z, 8), 1))
    row, col = iota((Z, Z), 0), iota((Z, Z), 1)
    same = row // 8 == col // 8
    line = mm(mm(low, closed), low, 1, 1) * where(same)
    line = line - penalty * where((jnp.abs(row - col) == 1) & ~same)
    return along_x + along_y, line


def start_kernel(scale, sums_ref, basis_ref, rhs_ref, inertia_ref, helm_ref, stiffness_ref,
                 coef_ref, x0_ref, q_ref, plane_ref, line_ref, up_ref, down_ref):
    plane, line = build(stiffness_ref[...])
    plane_ref[...] = plane
    line_ref[...] = line
    coef = jnp.sum(sums_ref[...], axis=0) * scale
    coef_ref[...] = coef
    x0 = jnp.concatenate([weighted(coef, basis_ref, s) for s in range(S)], axis=0)
    inertia = inertia_ref[...].reshape(X * Y, Z)
    q = rhs_ref[...].reshape(SXY, Z) - laplace(x0, inertia, helm_ref, plane, line)
    x0, q = x0.reshape(S, X, Y, Z), q.reshape(S, X, Y, Z)
    x0_ref[...] = x0
    q_ref[...] = q
    up_ref[0] = x0[:, X - 1]
    up_ref[1] = q[:, X - 1]
    down_ref[0] = x0[:, 0]
    down_ref[1] = q[:, 0]


def y_kernel(x0_ref, q_ref, xlo_ref, xhi_ref, up_ref, down_ref):
    for out_ref, y in ((up_ref, Y - 1), (down_ref, 0)):
        for s in range(S):
            low, high = xlo_ref[0, s, y:y + 1, :], xhi_ref[0, s, y:y + 1, :]
            for x in range(X):
                i = s * X + x
                out_ref[i:i + 1, :] = x0_ref[s, x, y:y + 1, :]
                q = q_ref[s, x, y:y + 1, :]
                if x == 0:
                    q = q + penalty * low
                if x == X - 1:
                    q = q + penalty * high
                out_ref[SX + i:SX + i + 1, :] = q
            out_ref[2 * SX + s:2 * SX + s + 1, :] = low
            out_ref[2 * SX + S + s:2 * SX + S + s + 1, :] = high


def z_kernel(x0_ref, q_ref, xlo_ref, xhi_ref, ylo_ref, yhi_ref, q2_ref, up_ref, down_ref):
    q = q_ref[...] + penalty * (at_x(xlo_ref[0], xhi_ref[0]) + at_y(ylo_ref[0:SX], yhi_ref[0:SX]))
    q2_ref[...] = q
    rows = jnp.concatenate(
        [x0_ref[...].reshape(SXY, Z), q.reshape(SXY, Z), xlo_ref[0].reshape(SX, Z), xhi_ref[0].reshape(SX, Z),
         ylo_ref[0:SX], yhi_ref[0:SX]], axis=0)
    picked = mm(ends(), rows, 1, 1)
    down_ref[...] = picked[0:1]
    up_ref[...] = picked[1:2]


def image_kernel(x0_ref, q2_ref, xlo_ref, xhi_ref, ylo_ref, yhi_ref, zlo_ref, zhi_ref, zup_ref, zdown_ref,
                 inside_ref, inertia_ref, helm_ref, plane_ref, line_ref,
                 r0_ref, v_ref, vx_ref, vy_ref, vz_ref, vz0_ref):
    zlo, zhi = zlo_ref[...], zhi_ref[...]
    put = spread(zlo, zhi)
    x0 = x0_ref[...]
    r0 = q2_ref[...].reshape(SXY, Z) + penalty * put[0:SXY]
    at = 2 * SXY
    rzl = inside_ref[4] * (zlo[:, SXY:at] + penalty * zdown_ref[:, 0:SXY])
    rzh = inside_ref[5] * (zhi[:, SXY:at] + penalty * zup_ref[:, 0:SXY])
    ends_y = []
    for y in (0, Y - 1):
        ends_y.append(jnp.concatenate(
            [x0_ref[s, x, y:y + 1, :] for s in range(S) for x in range(X)], axis=0))
    ryl = inside_ref[2] * (ylo_ref[SX:2 * SX] + penalty * (ends_y[0] + put[at + 2 * SX:at + 3 * SX]))
    ryh = inside_ref[3] * (yhi_ref[SX:2 * SX] + penalty * (ends_y[1] + put[at + 3 * SX:at + 4 * SX]))
    y = iota((S, Y, Z), 1)

    def layer(flag, q, own, first, columns):
        low, high = ylo_ref[first:first + S].reshape(S, 1, Z), yhi_ref[first:first + S].reshape(S, 1, Z)
        lines = jnp.where(y == 0, low, jnp.where(y == Y - 1, high, 0.0))
        return flag * (q + penalty * (own + lines + columns.reshape(S, Y, Z)))

    rxl = layer(inside_ref[0], xlo_ref[1], x0[:, 0], 2 * SX, put[at:at + SX])
    rxh = layer(inside_ref[1], xhi_ref[1], x0[:, X - 1], 2 * SX + S, put[at + SX:at + 2 * SX])
    around = at_x(rxl, rxh) + at_y(ryl, ryh)
    v = laplace(r0, inertia_ref[...].reshape(X * Y, Z), helm_ref, plane_ref[...], line_ref[...])
    v = v - penalty * (around.reshape(SXY, Z) + spread(rzl, rzh))
    picked = mm(ends(), v, 1, 1)
    vz0_ref[...] = picked[0:1]
    vz_ref[...] = picked[1:2]
    v = v.reshape(S, X, Y, Z)
    r0_ref[...] = r0.reshape(S, X, Y, Z)
    v_ref[...] = v
    vx_ref[...] = v[:, X - 1]
    for s in range(S):
        for x in range(X):
            vy_ref[s * X + x:s * X + x + 1, :] = v_ref[s, x, Y - 1:Y, :]


def moment_kernel(r0_ref, v_ref, basis_ref, inertia_ref, helm_ref, plane_ref, line_ref, out_ref):
    v_all = v_ref[...].reshape(SXY, Z)
    w_all = laplace(v_all, inertia_ref[...].reshape(X * Y, Z), helm_ref, plane_ref[...], line_ref[...])
    for s in range(S):
        r, v = r0_ref[s], v_ref[s]
        w = w_all[s * X * Y:(s + 1) * X * Y].reshape(X, Y, Z)
        at = 2 * SK + 4 * s
        for j, product in enumerate((r * r, r * v, v * v, v * w)):
            out_ref[at + j:at + j + 1, :] = row_sum(product)
        for k in range(K):
            b = basis_ref[s, k].astype(f32)
            i = s * K + k
            out_ref[i:i + 1, :] = row_sum(b * r)
            out_ref[SK + i:SK + i + 1, :] = row_sum(b * v)
            for d in range(DIAGONALS):
                at = 2 * SK + 16 + d * SK + i
                out_ref[at:at + 1, :] = row_sum(b * basis_ref[s, (k + d) % K].astype(f32))
    out_ref[ROWS:, :] = jnp.zeros((256 - ROWS, Z), f32)


def cross_kernel(rows_ref, v_ref, vz0_ref, xlo_ref, ylo_ref, zlo_ref, out_ref):
    rows = rows_ref[...]
    row = iota((256, Z), 0)
    z = vz0_ref[...] * zlo_ref[...]
    for s in range(S):
        crossing = jnp.sum(v_ref[s, 0] * xlo_ref[s], axis=0, keepdims=True)
        for x in range(X):
            crossing = crossing + v_ref[s, x, 0:1, :] * ylo_ref[s * X + x:s * X + x + 1, :]
        part = z[:, s * X * Y:(s + 1) * X * Y]
        crossing = crossing + jnp.concatenate([part, jnp.zeros((1, Z - X * Y), f32)], axis=1)
        rows = rows - jnp.where(row == 2 * SK + 4 * s + 3, 2.0 * penalty * crossing, 0.0)
    out_ref[...] = jnp.broadcast_to(lane_sums(rows)[None], out_ref.shape)


def final_kernel(scale, sums_ref, coef_ref, x0_ref, r0_ref, v_ref, basis_ref, out_ref, new_ref):
    sums = jnp.broadcast_to(jnp.sum(sums_ref[...], axis=0) * scale, (8, 256))
    g0, g1 = sums[:, 0:SK], sums[:, SK:2 * SK]
    powers = sums[:, 2 * SK:2 * SK + 16]
    row, col = iota((16, 4 * SK), 0), iota((16, 4 * SK), 1)
    powers = mm(powers, where(row == 4 * ((col % SK) // K) + col // SK))
    mu0, mu1, mu2, mu3 = (powers[:, j * SK:(j + 1) * SK] for j in range(4))
    gram = [sums[:, 2 * SK + 16 + d * SK:2 * SK + 16 + (d + 1) * SK] for d in range(DIAGONALS)]
    coef = jnp.broadcast_to(coef_ref[:, 0:SK], (8, SK))

    row, col = iota((SK, SK), 0), iota((SK, SK), 1)
    same = row // K == col // K
    turn = [where(same & ((col % K + d) % K == row % K)) for d in range(DIAGONALS)]
    back = [where(same & ((row % K + d) % K == col % K)) for d in range(DIAGONALS)]
    block = where(same)

    def gram_times(u):
        out = gram[0] * u
        for d in range(1, DIAGONALS):
            out = out + gram[d] * mm(u, turn[d])
        for d in range(1, DIAGONALS - 1):
            out = out + mm(gram[d] * u, back[d])
        return out

    step_0 = mu0 / mu1
    next_0 = jnp.maximum(step_0 * step_0 * mu2 - mu0, 0.0)
    grown = 1.0 + next_0 / mu0
    curvature = grown * grown * mu1 - 2.0 * grown * step_0 * mu2 + step_0 * step_0 * mu3
    step_1 = jnp.where(curvature * max_step > next_0, next_0 / curvature, max_step)
    of_r = step_0 + step_1 * grown
    of_v = -step_1 * step_0
    change = of_r * g0 + of_v * g1
    weights = gram_times(coef) + change
    left = coef - weights
    square = mm(left * gram_times(left) + 2.0 * left * change, block)
    square = square + of_r * of_r * mu0 + 2.0 * of_r * of_v * mu1 + of_v * of_v * mu2
    inverse = lax.rsqrt(square + epsilon)
    for s in range(S):
        at = s * K
        x = x0_ref[s].reshape(X * Y, Z) + column(of_r[0:1], at) * r0_ref[s].reshape(X * Y, Z)
        x = x + column(of_v[0:1], at) * v_ref[s].reshape(X * Y, Z)
        out_ref[s] = x.reshape(X, Y, Z)
        rest = (x - weighted(weights[0:1], basis_ref, s)) * column(inverse[0:1], at)
        new_ref[s] = rest.reshape(X, Y, Z).astype(jnp.bfloat16)


def shaped(*shape, dtype=f32):
    return jax.ShapeDtypeStruct(shape, dtype)


def call(kernel, outs, args, small=()):
    vmem, smem = pl.BlockSpec(memory_space=pltpu.VMEM), pl.BlockSpec(memory_space=pltpu.SMEM)
    return pl.pallas_call(
        kernel,
        out_shape=outs,
        in_specs=[smem if i in small else vmem for i in range(len(args))],
        out_specs=jax.tree.map(lambda _: vmem, outs),
    )(*args)


def total(copies):
    width = copies.shape[2]
    copies = lax.all_to_all(copies, PLANE, 0, 0)
    copies = call(fold_kernel, shaped(lax.axis_size(LINE), 1, width), (copies,))
    return lax.all_to_all(copies, LINE, 0, 0)


def upward(x, axis):
    return lax.ppermute(x, axis, [(i, i + 1) for i in range(lax.axis_size(axis) - 1)])


def downward(x, axis):
    return lax.ppermute(x, axis, [(i + 1, i) for i in range(lax.axis_size(axis) - 1)])


def on_device(rhs, basis, inertia, helm, stiffness):
    scale = 1.0 / float(rhs[0].size * lax.axis_size(PLANE + LINE))
    peers = lax.axis_size(PLANE)
    field = shaped(S, X, Y, Z)

    copies = call(coef_kernel, shaped(peers, 1, Z), (rhs, basis))
    sums = total(copies)

    def start(*refs):
        start_kernel(scale, *refs)

    coef, x0, q, plane, line, up, down = call(
        start,
        (shaped(1, Z), field, field, shaped(X * Y, X * Y), shaped(Z, Z), shaped(2, S, Y, Z), shaped(2, S, Y, Z)),
        (sums, basis, rhs, inertia, helm, stiffness), small=(4,))
    xlo, xhi = upward(up, GX), downward(down, GX)
    up, down = call(y_kernel, (shaped(2 * SX + 8, Z),) * 2, (x0, q, xlo, xhi))
    ylo, yhi = upward(up, "gy"), downward(down, "gy")
    q2, zup, zdown = call(
        z_kernel, (field, shaped(1, 640), shaped(1, 640)), (x0, q, xlo, xhi, ylo, yhi))
    zlo, zhi = upward(zup, "gz"), downward(zdown, "gz")

    places = [(lax.axis_index(axis), lax.axis_size(axis)) for axis in (GX, "gy", "gz")]
    inside = jnp.stack([jnp.where(test, 1.0, 0.0) for i, n in places for test in (i > 0, i < n - 1)])
    r0, v, vx, vy, vz, vz0 = call(
        image_kernel,
        (field, field, shaped(S, Y, Z), shaped(SX, Z), shaped(1, SXY), shaped(1, SXY)),
        (x0, q2, xlo, xhi, ylo, yhi, zlo, zhi, zup, zdown, inside, inertia, helm, plane, line), small=(10, 12))
    lows = [upward(a, axis) for a, axis in ((vx, GX), (vy, "gy"), (vz, "gz"))]
    rows = call(moment_kernel, shaped(256, Z), (r0, v, basis, inertia, helm, plane, line), small=(4,))
    copies = call(cross_kernel, shaped(peers, 1, 256), (rows, v, vz0, *lows))
    sums = total(copies)

    def final(*refs):
        final_kernel(scale, *refs)

    return call(final, (field, shaped(S, X, Y, Z, dtype=jnp.bfloat16)), (sums, coef, x0, r0, v, basis))


def solution(mesh):
    torus = Mesh(
        mesh.devices.reshape(mesh.shape["gx"] // 2, 2, mesh.shape["gy"], mesh.shape["gz"]),
        ("gx_0", "gx_1", "gy", "gz"),
    )
    placed = (P(None, GX, "gy", "gz"), P(None, None, GX, "gy", "gz"), P(GX, "gy", "gz"), P(), P())
    return jax.shard_map(
        on_device,
        mesh=torus,
        in_specs=placed,
        out_specs=(P(None, GX, "gy", "gz"), P(None, GX, "gy", "gz")),
        check_vma=False,
    )
```

time: 151 us -> 143 us (0.947)
  the two profiles are of different devices: /device:TPU:8 before, /device:TPU:2 now
where the time goes in v2:
time: 143 us; the launch traced here: 142 us
  blocking collectives  87 us (61%)
  Pallas kernels  22.8 us (16%)
  starting transfers between devices  19.7 us (14%)
  waiting for transfers between devices  9 us (6%)
  local copies, waits for them, and re-layouts  2.99 us (2%)
    all_to_all x2, blocking collectives, total(): copies = lax.all_to_all(copies, PLANE, 0, 0)  44.2 us
    all_to_all x2, blocking collectives, total(): return lax.all_to_all(copies, LINE, 0, 0)  42.8 us
    pallas_call x10, Pallas kernels, call(): pl.pallas_call(kernel, out_shape=outs, in_specs=[smem if i in small else...  22.8 us
    ppermute x6, starting transfers between devices, upward(): lax.ppermute(x, axis, [(i, i + 1) for i in range(lax.axis_size(axis) - 1)])  13.8 us
    ppermute x3, waiting for transfers between devices, downward(): lax.ppermute(x, axis, [(i + 1, i) for i in range(lax.axis_size(axis) - 1)])  8.35 us
    ppermute x3, starting transfers between devices, downward(): lax.ppermute(x, axis, [(i + 1, i) for i in range(lax.axis_size(axis) - 1)])  5.88 us
  transfers between devices with their start and end apart: 9, of which 4 were waited for; matrix products, arithmetic and copies ran while one was open for 0% of the time, Pallas kernels for 2%

profile of v2, /device:TPU:2, one launch (start us, length us, event | category | flops | bytes accessed | tf_op | source)
XLA Modules:
  0.0 142.3 jit_solution(7438465837107083897)
XLA Ops:
  0.6 2.0 %shard_map.68 = f32[64,1,128]{2,1,0:T(1,128)} custom-call(f32[4,8,8,128]{3,2,1,0:T(8,128)} %refs_2_.1, bf16[4,8,8,8,128]{4,3,2,1,0:T(8,128)(2,1)} %refs_5_.3), custom_call_target="tpu_custom_call" | custom-call | tf_op jit(solution)/shard_map/pallas_call | solution.py:294
  2.6 26.8 %all_to_all.20.in_ref = f32[64,1,128]{2,1,0:T(1,128)} all-to-all(f32[64,1,128]{2,1,0:T(1,128)} %shard_map.68), channel_id=1, replica_groups=mesh['gx_0'=8,'gx_1'=2,'gy'=16,'gz'=4] {'gx_0','gx_1','gz'}, dimensions={0} | all-to-all | bytes 65536 | tf_op jit(solution)/shard_map/all_to_all | solution.py:304
  29.4 1.4 %shard_map.69 = f32[16,1,128]{2,1,0:T(1,128)} custom-call(f32[64,1,128]{2,1,0:T(1,128)} %all_to_all.20.in_ref), custom_call_target="tpu_custom_call" | custom-call | tf_op jit(solution)/shard_map/pallas_call | solution.py:294
  30.8 23.9 %all_to_all.21.refs_0_ = f32[16,1,128]{2,1,0:T(1,128)} all-to-all(f32[16,1,128]{2,1,0:T(1,128)} %shard_map.69), channel_id=1, replica_groups=mesh['gx_0'=8,'gx_1'=2,'gy'=16,'gz'=4] {'gy'}, dimensions={0} | all-to-all | bytes 16384 | tf_op jit(solution)/shard_map/all_to_all | solution.py:306
  54.8 2.9 %shard_map.70 = (f32[1,128]{1,0:T(1,128)}, f32[4,8,8,128]{3,2,1,0:T(8,128)}, f32[4,8,8,128]{3,2,1,0:T(8,128)}, f32[64,64]{1,0:T(8,128)}, f32[128,128]{1,0:T(8,12...) custom-call(f32[16,1,128]{2,1,0:T(1,128)} %all_to_all.21.refs_0_, bf16[4,8,8,8,128]{4,3,2,1,0:T(8,128)(2,1)} %refs_5_.3, ...), custom_call_target="tpu_custom_call" | custom-call | tf_op jit(solution)/shard_map/pallas_call | solution.py:294
  57.6 1.3 collective-permute-start
  58.9 1.3 collective-permute-start.1
  60.2 0.0 collective-permute-done.xlo_ref
  60.2 0.0 copy-start
  60.2 2.7 %collective-permute-done.1.xhi_ref = f32[2,4,8,128]{3,2,1,0:T(8,128)S(1)} collective-permute-done((f32[2,4,8,128]{3,2,1,0:T(8,128)}, f32[2,4,8,128]{3,2,1,0:T(8,128)S(1)}, u32[]{:S(2)}, u32[]{:S(2)}) %collective-permute-start.1) | collective-permute-done | bytes 32800 | tf_op jit(solution)/shard_map/ppermute | solution.py:314
  62.9 0.0 copy-start.1
  62.9 0.0 copy-done
  62.9 0.6 copy-done.1
  63.5 1.7 %shard_map.71 = (f32[72,128]{1,0:T(8,128)}, f32[72,128]{1,0:T(8,128)}) custom-call(f32[4,8,8,128]{3,2,1,0:T(8,128)} %get-tuple-element.20.x0_ref.refs_2_, f32[4,8,8,128]{3,2,1,0:T(8,128)} %get-tuple-element.21.q_ref, f32[2,4,8,128]{3,2,1,0:T(8,128)} %copy-done, f32[2,4,8,128]{3,2,1,0:T(8,128)} %copy-done.1), custom_call_target="tpu_custom_call" | custom-call | tf_op jit(solution)/shard_map/pallas_call | solution.py:294
  65.2 2.5 %collective-permute-start.2 = (f32[72,128]{1,0:T(8,128)}, f32[72,128]{1,0:T(8,128)S(1)}, u32[]{:S(2)}, u32[]{:S(2)}) collective-permute-start(f32[72,128]{1,0:T(8,128)} %get-tuple-element.24), channel_id=1, source_target_pairs={{0,4},{4,8},{8,12},{12,16},{16,20},{20,24},{24,28},{28,32},{32,36}... | collective-permute-start | bytes 110600 | tf_op jit(solution)/shard_map/ppermute | solution.py:310
  67.7 1.3 collective-permute-start.3
  69.0 0.6 collective-permute-done.2.ylo_ref
  69.7 0.0 copy-start.2
  69.7 4.1 %collective-permute-done.3.yhi_ref = f32[72,128]{1,0:T(8,128)S(1)} collective-permute-done((f32[72,128]{1,0:T(8,128)}, f32[72,128]{1,0:T(8,128)S(1)}, u32[]{:S(2)}, u32[]{:S(2)}) %collective-permute-start.3) | collective-permute-done | bytes 36896 | tf_op jit(solution)/shard_map/ppermute | solution.py:314
  73.8 0.0 copy-done.2
  73.8 0.0 copy-start.3
  73.8 0.6 copy-done.3
  74.4 2.0 %shard_map.72 = (f32[4,8,8,128]{3,2,1,0:T(8,128)}, f32[1,640]{1,0:T(1,128)}, f32[1,640]{1,0:T(1,128)}) custom-call(f32[4,8,8,128]{3,2,1,0:T(8,128)} %get-tuple-element.20.x0_ref.refs_2_, f32[4,8,8,128]{3,2,1,0:T(8,128)} %get-tuple-element.21.q_ref, f32[2,4,8,128]{3,2,1,0:T(8,128)} %copy-done, f32[2,4,8,128]{3,2,1,0:T(8,128)} %copy-done.1, ...), custom_call_target="tpu_custom_call" | custom-call | tf_op jit(solution)/shard_map/pallas_call | solution.py:294
  76.4 0.0 copy-start.6
  76.4 2.7 %collective-permute-start.4 = (f32[1,640]{1,0:T(1,128)}, f32[1,640]{1,0:T(1,128)S(1)}, u32[]{:S(2)}, u32[]{:S(2)}) collective-permute-start(f32[1,640]{1,0:T(1,128)} %get-tuple-element.27.zup_ref), channel_id=1, source_target_pairs={{0,1},{1,2},{2,3},{4,5},{5,6},{6,7},{8,9},{9,10},{10,11},{12,13},{... | collective-permute-start | bytes 7688 | tf_op jit(solution)/shard_map/ppermute | solution.py:310
  79.1 0.0 copy-done.6
  79.1 3.3 %collective-permute-start.5 = (f32[1,640]{1,0:T(1,128)S(1)}, f32[1,640]{1,0:T(1,128)S(1)}, u32[]{:S(2)}, u32[]{:S(2)}) collective-permute-start(f32[1,640]{1,0:T(1,128)S(1)} %copy-done.6), channel_id=1, source_target_pairs={{1,0},{2,1},{3,2},{5,4},{6,5},{7,6},{9,8},{10,9},{11,10},{13,12},{... | collective-permute-start | bytes 7688 | tf_op jit(solution)/shard_map/ppermute | solution.py:314
  82.4 0.6 stack.27.inside_ref
  83.0 0.0 collective-permute-done.4.zlo_ref
  83.0 0.0 copy-start.7
  83.0 1.6 %collective-permute-done.5.zhi_ref = f32[1,640]{1,0:T(1,128)S(1)} collective-permute-done((f32[1,640]{1,0:T(1,128)S(1)}, f32[1,640]{1,0:T(1,128)S(1)}, u32[]{:S(2)}, u32[]{:S(2)}) %collective-permute-start.5) | collective-permute-done | bytes 2592 | tf_op jit(solution)/shard_map/ppermute | solution.py:314
  84.6 0.0 copy-start.8
  84.6 0.0 copy-done.7
  84.6 0.6 copy-done.8
  85.2 3.4 %shard_map.73 = (f32[4,8,8,128]{3,2,1,0:T(8,128)}, f32[4,8,8,128]{3,2,1,0:T(8,128)}, f32[4,8,128]{2,1,0:T(8,128)}, f32[32,128]{1,0:T(8,128)}, f32[1,256]{1,0:T(1,128)}, /*index=5*/f32[1,256]{1,0:T(1,128)}) custom-call(f32[4,8,8,128]{3,2,1,0:T(8,128)} %get-tuple-element.20.x0_ref.refs_2_, f32[4,8,8,128]{3,2,1,0:T(8,128)} %get-tuple-element.26.q2_ref, ...), custom_call_target="tpu_custom_call" | custom-call | tf_op jit(solution)/shard_map/pallas_call | solution.py:294
  88.5 1.7 %collective-permute-start.6 = (f32[4,8,128]{2,1,0:T(8,128)}, f32[4,8,128]{2,1,0:T(8,128)S(1)}, u32[]{:S(2)}, u32[]{:S(2)}) collective-permute-start(f32[4,8,128]{2,1,0:T(8,128)} %get-tuple-element.34), channel_id=1, source_target_pairs={{0,64},{64,128},{128,192},{192,256},{256,320},{320,384},{384,448},... | collective-permute-start | bytes 49160 | tf_op jit(solution)/shard_map/ppermute | solution.py:310
  90.2 0.0 copy-start.10
  90.2 2.5 %collective-permute-start.7 = (f32[32,128]{1,0:T(8,128)}, f32[32,128]{1,0:T(8,128)S(1)}, u32[]{:S(2)}, u32[]{:S(2)}) collective-permute-start(f32[32,128]{1,0:T(8,128)} %get-tuple-element.35), channel_id=1, source_target_pairs={{0,4},{4,8},{8,12},{12,16},{16,20},{20,24},{24,28},{28,32},{32,36}... | collective-permute-start | bytes 49160 | tf_op jit(solution)/shard_map/ppermute | solution.py:310
  92.7 0.0 copy-done.10
  92.7 3.2 %collective-permute-start.8 = (f32[1,256]{1,0:T(1,128)S(1)}, f32[1,256]{1,0:T(1,128)S(1)}, u32[]{:S(2)}, u32[]{:S(2)}) collective-permute-start(f32[1,256]{1,0:T(1,128)S(1)} %copy-done.10), channel_id=1, source_target_pairs={{0,1},{1,2},{2,3},{4,5},{5,6},{6,7},{8,9},{9,10},{10,11},{12,13},{... | collective-permute-start | bytes 3080 | tf_op jit(solution)/shard_map/ppermute | solution.py:310
  95.9 2.9 %shard_map.74.rows_ref = f32[256,128]{1,0:T(8,128)} custom-call(f32[4,8,8,128]{3,2,1,0:T(8,128)} %get-tuple-element.31.r0_ref.refs_3_, f32[4,8,8,128]{3,2,1,0:T(8,128)} %get-tuple-element.32.v_ref.refs_4_, bf16[4,8,8,8,128]{4,3,2,1,0:T(8,128)(2,1)} %refs_5_.3, f32[8,8,128]{2,1,0:T(8,128)} %inertia_ref.3, f32[4]{0:T(128)} %helm_ref.3, ...), custom_call_target="tpu_custom_call" | custom-call | tf_op jit(solution)/shard_map/pallas_call | solution.py:294
  98.8 0.0 collective-permute-done.8.zlo_ref
  98.8 0.0 copy-start.9
  98.8 0.0 collective-permute-done.6.xlo_ref
  98.8 0.0 copy-start.4
  98.8 0.0 collective-permute-done.7.ylo_ref
  98.8 0.0 copy-start.5
  98.8 0.5 copy-done.9
  99.4 0.0 copy-done.4
  99.4 0.0 copy-done.5
  99.4 1.9 %shard_map.75 = f32[64,1,256]{2,1,0:T(1,128)} custom-call(f32[256,128]{1,0:T(8,128)} %shard_map.74.rows_ref, f32[4,8,8,128]{3,2,1,0:T(8,128)} %get-tuple-element.32.v_ref.refs_4_, f32[1,256]{1,0:T(1,128)} %get-tuple-element.33.vz0_ref, f32[4,8,128]{2,1,0:T(8,128)} %copy-done.4, f32[32,128]{1,0:T(8,128)} %copy-done.5, f32[1,256]{1,0:T(1,128)} %copy-done.9), custom_call_target="tpu_custom_call" | custom-call | tf_op jit(solution)/shard_map/pallas_call | solution.py:294
  101.3 17.4 %all_to_all.22.in_ref = f32[64,1,256]{2,1,0:T(1,128)} all-to-all(f32[64,1,256]{2,1,0:T(1,128)} %shard_map.75), channel_id=1, replica_groups=mesh['gx_0'=8,'gx_1'=2,'gy'=16,'gz'=4] {'gx_0','gx_1','gz'}, dimensions={0} | all-to-all | bytes 131072 | tf_op jit(solution)/shard_map/all_to_all | solution.py:304
  118.8 1.5 %shard_map.76 = f32[16,1,256]{2,1,0:T(1,128)} custom-call(f32[64,1,256]{2,1,0:T(1,128)} %all_to_all.22.in_ref), custom_call_target="tpu_custom_call" | custom-call | tf_op jit(solution)/shard_map/pallas_call | solution.py:294
  120.3 18.9 %all_to_all.23.refs_0_ = f32[16,1,256]{2,1,0:T(1,128)} all-to-all(f32[16,1,256]{2,1,0:T(1,128)} %shard_map.76), channel_id=1, replica_groups=mesh['gx_0'=8,'gx_1'=2,'gy'=16,'gz'=4] {'gy'}, dimensions={0} | all-to-all | bytes 32768 | tf_op jit(solution)/shard_map/all_to_all | solution.py:306
  139.2 3.2 %shard_map.77 = (f32[4,8,8,128]{3,2,1,0:T(8,128)}, bf16[4,8,8,128]{3,2,1,0:T(8,128)(2,1)}) custom-call(f32[16,1,256]{2,1,0:T(1,128)} %all_to_all.23.refs_0_, f32[1,128]{1,0:T(1,128)} %get-tuple-element.37.refs_1_, f32[4,8,8,128]{3,2,1,0:T(8,128)} %get-tuple-element.20.x0_ref.refs_2_, f32[4,8,8,128]{3,2,1,0:T(8,128)} %get-tuple-element.31.r0_ref.refs_3_, ...), custom_call_target="tpu_custom_call" | custom-call | tf_op jit(solution)/shard_map/pallas_call | solution.py:294
Async XLA Ops:
  57.6 2.6 %collective-permute-start = (f32[2,4,8,128]{3,2,1,0:T(8,128)}, f32[2,4,8,128]{3,2,1,0:T(8,128)S(1)}, u32[]{:S(2)}, u32[]{:S(2)}) collective-permute-start(f32[2,4,8,128]{3,2,1,0:T(8,128)} %get-tuple-element.22), channel_id=1, source_target_pairs={{0,64},{64,128},{128,192},{192,256},{256,320},{320,384},{384,448},... | collective-permute-start | bytes 98312 | tf_op jit(solution)/shard_map/ppermute | solution.py:310
  58.9 4.0 %collective-permute-start.1 = (f32[2,4,8,128]{3,2,1,0:T(8,128)}, f32[2,4,8,128]{3,2,1,0:T(8,128)S(1)}, u32[]{:S(2)}, u32[]{:S(2)}) collective-permute-start(f32[2,4,8,128]{3,2,1,0:T(8,128)} %get-tuple-element.23), channel_id=1, source_target_pairs={{64,0},{128,64},{192,128},{256,192},{320,256},{384,320},{448,384},... | collective-permute-start | bytes 98312 | tf_op jit(solution)/shard_map/ppermute | solution.py:314
  60.2 2.7 %copy-start = (f32[2,4,8,128]{3,2,1,0:T(8,128)}, f32[2,4,8,128]{3,2,1,0:T(8,128)S(1)}, u32[]{:S(2)}) copy-start(f32[2,4,8,128]{3,2,1,0:T(8,128)S(1)} %collective-permute-done.xlo_ref) | copy-start | bytes 98308
  62.9 0.6 copy-start.1
  65.2 4.5 %collective-permute-start.2 = (f32[72,128]{1,0:T(8,128)}, f32[72,128]{1,0:T(8,128)S(1)}, u32[]{:S(2)}, u32[]{:S(2)}) collective-permute-start(f32[72,128]{1,0:T(8,128)} %get-tuple-element.24), channel_id=1, source_target_pairs={{0,4},{4,8},{8,12},{12,16},{16,20},{20,24},{24,28},{28,32},{32,36}... | collective-permute-start | bytes 110600 | tf_op jit(solution)/shard_map/ppermute | solution.py:310
  67.7 6.1 %collective-permute-start.3 = (f32[72,128]{1,0:T(8,128)}, f32[72,128]{1,0:T(8,128)S(1)}, u32[]{:S(2)}, u32[]{:S(2)}) collective-permute-start(f32[72,128]{1,0:T(8,128)} %get-tuple-element.25), channel_id=1, source_target_pairs={{4,0},{8,4},{12,8},{16,12},{20,16},{24,20},{28,24},{32,28},{36,32}... | collective-permute-start | bytes 110600 | tf_op jit(solution)/shard_map/ppermute | solution.py:314
  69.7 4.1 %copy-start.2 = (f32[72,128]{1,0:T(8,128)}, f32[72,128]{1,0:T(8,128)S(1)}, u32[]{:S(2)}) copy-start(f32[72,128]{1,0:T(8,128)S(1)} %collective-permute-done.2.ylo_ref) | copy-start | bytes 110596
  73.8 0.6 copy-start.3
  76.4 2.7 %copy-start.6 = (f32[1,640]{1,0:T(1,128)S(1)}, f32[1,640]{1,0:T(1,128)}, u32[]{:S(2)}) copy-start(f32[1,640]{1,0:T(1,128)} %get-tuple-element.28.zdown_ref) | copy-start | bytes 7684
  76.4 6.6 %collective-permute-start.4 = (f32[1,640]{1,0:T(1,128)}, f32[1,640]{1,0:T(1,128)S(1)}, u32[]{:S(2)}, u32[]{:S(2)}) collective-permute-start(f32[1,640]{1,0:T(1,128)} %get-tuple-element.27.zup_ref), channel_id=1, source_target_pairs={{0,1},{1,2},{2,3},{4,5},{5,6},{6,7},{8,9},{9,10},{10,11},{12,13},{... | collective-permute-start | bytes 7688 | tf_op jit(solution)/shard_map/ppermute | solution.py:310
  79.1 5.5 %collective-permute-start.5 = (f32[1,640]{1,0:T(1,128)S(1)}, f32[1,640]{1,0:T(1,128)S(1)}, u32[]{:S(2)}, u32[]{:S(2)}) collective-permute-start(f32[1,640]{1,0:T(1,128)S(1)} %copy-done.6), channel_id=1, source_target_pairs={{1,0},{2,1},{3,2},{5,4},{6,5},{7,6},{9,8},{10,9},{11,10},{13,12},{... | collective-permute-start | bytes 7688 | tf_op jit(solution)/shard_map/ppermute | solution.py:314
  83.0 1.6 %copy-start.7 = (f32[1,640]{1,0:T(1,128)}, f32[1,640]{1,0:T(1,128)S(1)}, u32[]{:S(2)}) copy-start(f32[1,640]{1,0:T(1,128)S(1)} %collective-permute-done.4.zlo_ref) | copy-start | bytes 7684
  84.6 0.6 copy-start.8
  88.5 10.3 %collective-permute-start.6 = (f32[4,8,128]{2,1,0:T(8,128)}, f32[4,8,128]{2,1,0:T(8,128)S(1)}, u32[]{:S(2)}, u32[]{:S(2)}) collective-permute-start(f32[4,8,128]{2,1,0:T(8,128)} %get-tuple-element.34), channel_id=1, source_target_pairs={{0,64},{64,128},{128,192},{192,256},{256,320},{320,384},{384,448},... | collective-permute-start | bytes 49160 | tf_op jit(solution)/shard_map/ppermute | solution.py:310
  90.2 2.5 %copy-start.10 = (f32[1,256]{1,0:T(1,128)S(1)}, f32[1,256]{1,0:T(1,128)}, u32[]{:S(2)}) copy-start(f32[1,256]{1,0:T(1,128)} %get-tuple-element.36) | copy-start | bytes 3076
  90.2 8.6 %collective-permute-start.7 = (f32[32,128]{1,0:T(8,128)}, f32[32,128]{1,0:T(8,128)S(1)}, u32[]{:S(2)}, u32[]{:S(2)}) collective-permute-start(f32[32,128]{1,0:T(8,128)} %get-tuple-element.35), channel_id=1, source_target_pairs={{0,4},{4,8},{8,12},{12,16},{16,20},{20,24},{24,28},{28,32},{32,36}... | collective-permute-start | bytes 49160 | tf_op jit(solution)/shard_map/ppermute | solution.py:310
  92.7 6.1 %collective-permute-start.8 = (f32[1,256]{1,0:T(1,128)S(1)}, f32[1,256]{1,0:T(1,128)S(1)}, u32[]{:S(2)}, u32[]{:S(2)}) collective-permute-start(f32[1,256]{1,0:T(1,128)S(1)} %copy-done.10), channel_id=1, source_target_pairs={{0,1},{1,2},{2,3},{4,5},{5,6},{6,7},{8,9},{9,10},{10,11},{12,13},{... | collective-permute-start | bytes 3080 | tf_op jit(solution)/shard_map/ppermute | solution.py:310
  98.8 0.6 copy-start.9
  98.8 0.6 copy-start.4
  98.8 0.6 copy-start.5

commit v3 on v2

--- a/solution.py
+++ b/solution.py
@@ -289,13 +289,17 @@
     return jax.ShapeDtypeStruct(shape, dtype)
 
 
-def call(kernel, outs, args, small=()):
+def call(kernel, outs, args, small=(), last=False):
     vmem, smem = pl.BlockSpec(memory_space=pltpu.VMEM), pl.BlockSpec(memory_space=pltpu.SMEM)
+    specs = jax.tree.map(lambda _: vmem, outs)
+    if not last:
+        outs = jax.tree.map(lambda out: pltpu.VMEM(out.shape, out.dtype), outs)
+    args = [a if i in small else pltpu.with_memory_space_constraint(a, pltpu.VMEM) for i, a in enumerate(args)]
     return pl.pallas_call(
         kernel,
         out_shape=outs,
         in_specs=[smem if i in small else vmem for i in range(len(args))],
-        out_specs=jax.tree.map(lambda _: vmem, outs),
+        out_specs=specs,
     )(*args)
 
 
@@ -350,7 +354,7 @@
     def final(*refs):
         final_kernel(scale, *refs)
 
-    return call(final, (field, shaped(S, X, Y, Z, dtype=jnp.bfloat16)), (sums, coef, x0, r0, v, basis))
+    return call(final, (field, shaped(S, X, Y, Z, dtype=jnp.bfloat16)), (sums, coef, x0, r0, v, basis), last=True)
 
 
 def solution(mesh):

time: 143 us -> 128 us (0.90)
  the two profiles are of different devices: /device:TPU:2 before, /device:TPU:8 now
where the time goes in v3:
time: 128 us
  blocking collectives  85.7 us (67%)
  starting transfers between devices  20.1 us (16%)
  waiting for transfers between devices  9.65 us (8%)
  Pallas kernels  8.87 us (7%)
  local copies, waits for them, and re-layouts  2.59 us (2%)
    all_to_all x2, blocking collectives, total(): return lax.all_to_all(copies, LINE, 0, 0)  43.6 us
    all_to_all x2, blocking collectives, total(): copies = lax.all_to_all(copies, PLANE, 0, 0)  42 us
    ppermute x6, starting transfers between devices, upward(): lax.ppermute(x, axis, [(i, i + 1) for i in range(lax.axis_size(axis) - 1)])  13.9 us
    ppermute x3, waiting for transfers between devices, downward(): lax.ppermute(x, axis, [(i + 1, i) for i in range(lax.axis_size(axis) - 1)])  9.32 us
    pallas_call x10, Pallas kernels, call(): pl.pallas_call(kernel, out_shape=outs, in_specs=[smem if i in small else...  8.87 us
    ppermute x3, starting transfers between devices, downward(): lax.ppermute(x, axis, [(i + 1, i) for i in range(lax.axis_size(axis) - 1)])  6.23 us
  transfers between devices with their start and end apart: 9, of which 4 were waited for; matrix products, arithmetic and copies ran while one was open for 0% of the time, Pallas kernels for 1%

profile of v3, /device:TPU:8, one launch (start us, length us, event | category | flops | bytes accessed | tf_op | source)
XLA Modules:
  0.0 127.7 jit_solution(17150016493470509040)
XLA Ops:
  0.6 0.0 copy-start
  0.6 1.0 copy-done
  1.7 0.0 copy-start.2
  1.7 0.9 copy-done.2
  2.6 0.0 copy-start.3
  2.6 0.3 shard_map.68
  2.9 25.1 %all_to_all.20.in_ref = f32[64,1,128]{2,1,0:T(1,128)S(1)} all-to-all(f32[64,1,128]{2,1,0:T(1,128)S(1)} %shard_map.68), channel_id=1, replica_groups=mesh['gx_0'=8,'gx_1'=2,'gy'=16,'gz'=4] {'gx_0','gx_1','gz'}, dimensions={0} | all-to-all | bytes 65536 | tf_op jit(solution)/shard_map/all_to_all | solution.py:308
  28.0 0.0 copy-start.4
  28.0 0.1 shard_map.69
  28.1 0.0 copy-start.5
  28.1 25.1 %all_to_all.21.refs_0_ = f32[16,1,128]{2,1,0:T(1,128)S(1)} all-to-all(f32[16,1,128]{2,1,0:T(1,128)S(1)} %shard_map.69), channel_id=1, replica_groups=mesh['gx_0'=8,'gx_1'=2,'gy'=16,'gz'=4] {'gy'}, dimensions={0} | all-to-all | bytes 16384 | tf_op jit(solution)/shard_map/all_to_all | solution.py:310
  53.2 0.0 copy-done.3
  53.2 0.0 copy-done.4
  53.2 0.0 copy-done.5
  53.2 1.7 %shard_map.70 = (f32[1,128]{1,0:T(1,128)S(1)}, f32[4,8,8,128]{3,2,1,0:T(8,128)S(1)}, f32[4,8,8,128]{3,2,1,0:T(8,128)S(1)}, f32[64,64]{1,0:T(8,128)S(1)}, f32[128...) custom-call(f32[16,1,128]{2,1,0:T(1,128)S(1)} %all_to_all.21.refs_0_, ...), custom_call_target="tpu_custom_call" | custom-call | tf_op jit(solution)/shard_map/pallas_call | solution.py:298
  54.9 1.9 %collective-permute-start = (f32[2,4,8,128]{3,2,1,0:T(8,128)S(1)}, f32[2,4,8,128]{3,2,1,0:T(8,128)S(1)}, u32[]{:S(2)}, u32[]{:S(2)}) collective-permute-start(f32[2,4,8,128]{3,2,1,0:T(8,128)S(1)} %get-tuple-element.22), channel_id=1, source_target_pairs={{0,64},{64,128},{128,192},{192,256},{256,320},{320,384},{384,448},... | collective-permute-start | bytes 98312 | tf_op jit(solution)/shard_map/ppermute | solution.py:314
  56.9 3.6 %collective-permute-start.1 = (f32[2,4,8,128]{3,2,1,0:T(8,128)S(1)}, f32[2,4,8,128]{3,2,1,0:T(8,128)S(1)}, u32[]{:S(2)}, u32[]{:S(2)}) collective-permute-start(f32[2,4,8,128]{3,2,1,0:T(8,128)S(1)} %get-tuple-element.23), channel_id=1, source_target_pairs={{64,0},{128,64},{192,128},{256,192},{320,256},{384,320},{448,384},... | collective-permute-start | bytes 98312 | tf_op jit(solution)/shard_map/ppermute | solution.py:318
  60.5 0.0 collective-permute-done.xlo_ref
  60.5 1.6 %collective-permute-done.1.xhi_ref = f32[2,4,8,128]{3,2,1,0:T(8,128)S(1)} collective-permute-done((f32[2,4,8,128]{3,2,1,0:T(8,128)S(1)}, f32[2,4,8,128]{3,2,1,0:T(8,128)S(1)}, u32[]{:S(2)}, u32[]{:S(2)}) %collective-permute-start.1) | collective-permute-done | bytes 32800 | tf_op jit(solution)/shard_map/ppermute | solution.py:318
  62.1 0.1 shard_map.71
  62.1 0.0 copy-start.1
  62.2 2.6 %collective-permute-start.2 = (f32[72,128]{1,0:T(8,128)S(1)}, f32[72,128]{1,0:T(8,128)S(1)}, u32[]{:S(2)}, u32[]{:S(2)}) collective-permute-start(f32[72,128]{1,0:T(8,128)S(1)} %get-tuple-element.24), channel_id=1, source_target_pairs={{0,4},{4,8},{8,12},{12,16},{16,20},{20,24},{24,28},{28,32},{32,36}... | collective-permute-start | bytes 110600 | tf_op jit(solution)/shard_map/ppermute | solution.py:314
  64.8 1.3 %collective-permute-start.3 = (f32[72,128]{1,0:T(8,128)S(1)}, f32[72,128]{1,0:T(8,128)S(1)}, u32[]{:S(2)}, u32[]{:S(2)}) collective-permute-start(f32[72,128]{1,0:T(8,128)S(1)} %get-tuple-element.25), channel_id=1, source_target_pairs={{4,0},{8,4},{12,8},{16,12},{20,16},{24,20},{28,24},{32,28},{36,32}... | collective-permute-start | bytes 110600 | tf_op jit(solution)/shard_map/ppermute | solution.py:318
  66.1 0.3 collective-permute-done.2.ylo_ref
  66.4 4.2 %collective-permute-done.3.yhi_ref = f32[72,128]{1,0:T(8,128)S(1)} collective-permute-done((f32[72,128]{1,0:T(8,128)S(1)}, f32[72,128]{1,0:T(8,128)S(1)}, u32[]{:S(2)}, u32[]{:S(2)}) %collective-permute-start.3) | collective-permute-done | bytes 36896 | tf_op jit(solution)/shard_map/ppermute | solution.py:318
  70.7 0.4 shard_map.72
  71.1 2.5 %collective-permute-start.4 = (f32[1,640]{1,0:T(1,128)S(1)}, f32[1,640]{1,0:T(1,128)S(1)}, u32[]{:S(2)}, u32[]{:S(2)}) collective-permute-start(f32[1,640]{1,0:T(1,128)S(1)} %get-tuple-element.27.zup_ref), channel_id=1, source_target_pairs={{0,1},{1,2},{2,3},{4,5},{5,6},{6,7},{8,9},{9,10},{10,11},{12,13},{... | collective-permute-start | bytes 7688 | tf_op jit(solution)/shard_map/ppermute | solution.py:314
  73.6 1.3 %collective-permute-start.5 = (f32[1,640]{1,0:T(1,128)S(1)}, f32[1,640]{1,0:T(1,128)S(1)}, u32[]{:S(2)}, u32[]{:S(2)}) collective-permute-start(f32[1,640]{1,0:T(1,128)S(1)} %get-tuple-element.28.zdown_ref), channel_id=1, source_target_pairs={{1,0},{2,1},{3,2},{5,4},{6,5},{7,6},{9,8},{10,9},{11,10},{13,12},{... | collective-permute-start | bytes 7688 | tf_op jit(solution)/shard_map/ppermute | solution.py:318
  74.9 0.6 stack.27.inside_ref
  75.5 0.0 collective-permute-done.4.zlo_ref
  75.5 3.5 %collective-permute-done.5.zhi_ref = f32[1,640]{1,0:T(1,128)S(1)} collective-permute-done((f32[1,640]{1,0:T(1,128)S(1)}, f32[1,640]{1,0:T(1,128)S(1)}, u32[]{:S(2)}, u32[]{:S(2)}) %collective-permute-start.5) | collective-permute-done | bytes 2592 | tf_op jit(solution)/shard_map/ppermute | solution.py:318
  79.1 2.3 %shard_map.73 = (f32[4,8,8,128]{3,2,1,0:T(8,128)S(1)}, f32[4,8,8,128]{3,2,1,0:T(8,128)S(1)}, f32[4,8,128]{2,1,0:T(8,128)S(1)}, f32[32,128]{1,0:T(8,128)S(1)}, f3...) custom-call(f32[4,8,8,128]{3,2,1,0:T(8,128)S(1)} %get-tuple-element.20.x0_ref.refs_2_, ...), custom_call_target="tpu_custom_call" | custom-call | tf_op jit(solution)/shard_map/pallas_call | solution.py:298
  81.4 1.9 %collective-permute-start.6 = (f32[4,8,128]{2,1,0:T(8,128)S(1)}, f32[4,8,128]{2,1,0:T(8,128)S(1)}, u32[]{:S(2)}, u32[]{:S(2)}) collective-permute-start(f32[4,8,128]{2,1,0:T(8,128)S(1)} %get-tuple-element.34), channel_id=1, source_target_pairs={{0,64},{64,128},{128,192},{192,256},{256,320},{320,384},{384,448},... | collective-permute-start | bytes 49160 | tf_op jit(solution)/shard_map/ppermute | solution.py:314
  83.3 2.4 %collective-permute-start.7 = (f32[32,128]{1,0:T(8,128)S(1)}, f32[32,128]{1,0:T(8,128)S(1)}, u32[]{:S(2)}, u32[]{:S(2)}) collective-permute-start(f32[32,128]{1,0:T(8,128)S(1)} %get-tuple-element.35), channel_id=1, source_target_pairs={{0,4},{4,8},{8,12},{12,16},{16,20},{20,24},{24,28},{28,32},{32,36}... | collective-permute-start | bytes 49160 | tf_op jit(solution)/shard_map/ppermute | solution.py:314
  85.7 2.5 %collective-permute-start.8 = (f32[1,256]{1,0:T(1,128)S(1)}, f32[1,256]{1,0:T(1,128)S(1)}, u32[]{:S(2)}, u32[]{:S(2)}) collective-permute-start(f32[1,256]{1,0:T(1,128)S(1)} %get-tuple-element.36), channel_id=1, source_target_pairs={{0,1},{1,2},{2,3},{4,5},{5,6},{6,7},{8,9},{9,10},{10,11},{12,13},{... | collective-permute-start | bytes 3080 | tf_op jit(solution)/shard_map/ppermute | solution.py:314
  88.2 0.0 copy-done.1
  88.3 1.7 %shard_map.74.rows_ref = f32[256,128]{1,0:T(8,128)S(1)} custom-call(f32[4,8,8,128]{3,2,1,0:T(8,128)S(1)} %get-tuple-element.31.r0_ref.refs_3_, f32[4,8,8,128]{3,2,1,0:T(8,128)S(1)} %get-tuple-element.32.v_ref.refs_4_, bf16[4,8,8,8,128]{4,3,2,1,0:T(8,128)(2,1)S(1)} %copy-done.1, f32[8,8,128]{2,1,0:T(8,128)S(1)} %copy-done.4, f32[4]{0:T(128)} %helm_ref.3, ...), custom_call_target="tpu_custom_call" | custom-call | tf_op jit(solution)/shard_map/pallas_call | solution.py:298
  89.9 0.0 collective-permute-done.8.zlo_ref
  90.0 0.0 collective-permute-done.6.xlo_ref
  90.0 0.0 collective-permute-done.7.ylo_ref
  90.0 0.3 shard_map.75
  90.3 16.9 %all_to_all.22.in_ref = f32[64,1,256]{2,1,0:T(1,128)S(1)} all-to-all(f32[64,1,256]{2,1,0:T(1,128)S(1)} %shard_map.75), channel_id=1, replica_groups=mesh['gx_0'=8,'gx_1'=2,'gy'=16,'gz'=4] {'gx_0','gx_1','gz'}, dimensions={0} | all-to-all | bytes 131072 | tf_op jit(solution)/shard_map/all_to_all | solution.py:308
  107.2 0.1 shard_map.76
  107.3 18.6 %all_to_all.23.refs_0_ = f32[16,1,256]{2,1,0:T(1,128)S(1)} all-to-all(f32[16,1,256]{2,1,0:T(1,128)S(1)} %shard_map.76), channel_id=1, replica_groups=mesh['gx_0'=8,'gx_1'=2,'gy'=16,'gz'=4] {'gy'}, dimensions={0} | all-to-all | bytes 32768 | tf_op jit(solution)/shard_map/all_to_all | solution.py:310
  125.8 1.9 %shard_map.77 = (f32[4,8,8,128]{3,2,1,0:T(8,128)}, bf16[4,8,8,128]{3,2,1,0:T(8,128)(2,1)}) custom-call(f32[16,1,256]{2,1,0:T(1,128)S(1)} %all_to_all.23.refs_0_, f32[1,128]{1,0:T(1,128)S(1)} %get-tuple-element.37.refs_1_, f32[4,8,8,128]{3,2,1,0:T(8,128)S(1)} %get-tuple-element.20.x0_ref.refs_2_, f32[4,8,8,128]{3,2,1,0:T(8,128)S(1)} %get-tuple-element.31.r0_ref.refs_3_, ...), custom_call_target="tpu_custom_call" | custom-call | tf_op jit(solution)/shard_map/pallas_call | solution.py:298
Async XLA Ops:
  0.6 1.0 copy-start
  1.7 0.9 copy-start.2
  2.6 50.6 %copy-start.3 = (f32[4,8,8,128]{3,2,1,0:T(8,128)S(1)}, f32[4,8,8,128]{3,2,1,0:T(8,128)}, u32[]{:S(2)}) copy-start(f32[4,8,8,128]{3,2,1,0:T(8,128)} %refs_2_.1) | copy-start | bytes 393220
  28.0 25.2 %copy-start.4 = (f32[8,8,128]{2,1,0:T(8,128)S(1)}, f32[8,8,128]{2,1,0:T(8,128)}, u32[]{:S(2)}) copy-start(f32[8,8,128]{2,1,0:T(8,128)} %inertia_ref.3) | copy-start | bytes 98308
  28.1 25.1 %copy-start.5 = (f32[8,8]{1,0:T(8,128)S(1)}, f32[8,8]{1,0:T(8,128)}, u32[]{:S(2)}) copy-start(f32[8,8]{1,0:T(8,128)} %refs_5_.2) | copy-start | bytes 772
  54.9 5.6 %collective-permute-start = (f32[2,4,8,128]{3,2,1,0:T(8,128)S(1)}, f32[2,4,8,128]{3,2,1,0:T(8,128)S(1)}, u32[]{:S(2)}, u32[]{:S(2)}) collective-permute-start(f32[2,4,8,128]{3,2,1,0:T(8,128)S(1)} %get-tuple-element.22), channel_id=1, source_target_pairs={{0,64},{64,128},{128,192},{192,256},{256,320},{320,384},{384,448},... | collective-permute-start | bytes 98312 | tf_op jit(solution)/shard_map/ppermute | solution.py:314
  56.9 5.2 %collective-permute-start.1 = (f32[2,4,8,128]{3,2,1,0:T(8,128)S(1)}, f32[2,4,8,128]{3,2,1,0:T(8,128)S(1)}, u32[]{:S(2)}, u32[]{:S(2)}) collective-permute-start(f32[2,4,8,128]{3,2,1,0:T(8,128)S(1)} %get-tuple-element.23), channel_id=1, source_target_pairs={{64,0},{128,64},{192,128},{256,192},{320,256},{384,320},{448,384},... | collective-permute-start | bytes 98312 | tf_op jit(solution)/shard_map/ppermute | solution.py:318
  62.1 26.1 %copy-start.1 = (bf16[4,8,8,8,128]{4,3,2,1,0:T(8,128)(2,1)S(1)}, bf16[4,8,8,8,128]{4,3,2,1,0:T(8,128)(2,1)}, u32[]{:S(2)}) copy-start(bf16[4,8,8,8,128]{4,3,2,1,0:T(8,128)(2,1)} %refs_5_.3) | copy-start | bytes 1572868
  62.2 4.3 %collective-permute-start.2 = (f32[72,128]{1,0:T(8,128)S(1)}, f32[72,128]{1,0:T(8,128)S(1)}, u32[]{:S(2)}, u32[]{:S(2)}) collective-permute-start(f32[72,128]{1,0:T(8,128)S(1)} %get-tuple-element.24), channel_id=1, source_target_pairs={{0,4},{4,8},{8,12},{12,16},{16,20},{20,24},{24,28},{28,32},{32,36}... | collective-permute-start | bytes 110600 | tf_op jit(solution)/shard_map/ppermute | solution.py:314
  64.8 5.9 %collective-permute-start.3 = (f32[72,128]{1,0:T(8,128)S(1)}, f32[72,128]{1,0:T(8,128)S(1)}, u32[]{:S(2)}, u32[]{:S(2)}) collective-permute-start(f32[72,128]{1,0:T(8,128)S(1)} %get-tuple-element.25), channel_id=1, source_target_pairs={{4,0},{8,4},{12,8},{16,12},{20,16},{24,20},{28,24},{32,28},{36,32}... | collective-permute-start | bytes 110600 | tf_op jit(solution)/shard_map/ppermute | solution.py:318
  71.1 4.5 %collective-permute-start.4 = (f32[1,640]{1,0:T(1,128)S(1)}, f32[1,640]{1,0:T(1,128)S(1)}, u32[]{:S(2)}, u32[]{:S(2)}) collective-permute-start(f32[1,640]{1,0:T(1,128)S(1)} %get-tuple-element.27.zup_ref), channel_id=1, source_target_pairs={{0,1},{1,2},{2,3},{4,5},{5,6},{6,7},{8,9},{9,10},{10,11},{12,13},{... | collective-permute-start | bytes 7688 | tf_op jit(solution)/shard_map/ppermute | solution.py:314
  73.6 5.5 %collective-permute-start.5 = (f32[1,640]{1,0:T(1,128)S(1)}, f32[1,640]{1,0:T(1,128)S(1)}, u32[]{:S(2)}, u32[]{:S(2)}) collective-permute-start(f32[1,640]{1,0:T(1,128)S(1)} %get-tuple-element.28.zdown_ref), channel_id=1, source_target_pairs={{1,0},{2,1},{3,2},{5,4},{6,5},{7,6},{9,8},{10,9},{11,10},{13,12},{... | collective-permute-start | bytes 7688 | tf_op jit(solution)/shard_map/ppermute | solution.py:318
  81.4 8.6 %collective-permute-start.6 = (f32[4,8,128]{2,1,0:T(8,128)S(1)}, f32[4,8,128]{2,1,0:T(8,128)S(1)}, u32[]{:S(2)}, u32[]{:S(2)}) collective-permute-start(f32[4,8,128]{2,1,0:T(8,128)S(1)} %get-tuple-element.34), channel_id=1, source_target_pairs={{0,64},{64,128},{128,192},{192,256},{256,320},{320,384},{384,448},... | collective-permute-start | bytes 49160 | tf_op jit(solution)/shard_map/ppermute | solution.py:314
  83.3 6.6 %collective-permute-start.7 = (f32[32,128]{1,0:T(8,128)S(1)}, f32[32,128]{1,0:T(8,128)S(1)}, u32[]{:S(2)}, u32[]{:S(2)}) collective-permute-start(f32[32,128]{1,0:T(8,128)S(1)} %get-tuple-element.35), channel_id=1, source_target_pairs={{0,4},{4,8},{8,12},{12,16},{16,20},{20,24},{24,28},{28,32},{32,36}... | collective-permute-start | bytes 49160 | tf_op jit(solution)/shard_map/ppermute | solution.py:314
  85.7 4.2 %collective-permute-start.8 = (f32[1,256]{1,0:T(1,128)S(1)}, f32[1,256]{1,0:T(1,128)S(1)}, u32[]{:S(2)}, u32[]{:S(2)}) collective-permute-start(f32[1,256]{1,0:T(1,128)S(1)} %get-tuple-element.36), channel_id=1, source_target_pairs={{0,1},{1,2},{2,3},{4,5},{5,6},{6,7},{8,9},{9,10},{10,11},{12,13},{... | collective-permute-start | bytes 3080 | tf_op jit(solution)/shard_map/ppermute | solution.py:314
